TPU v7x, 32 devices: a whole 2x2x4 slice. The times are simulated.
32 devices in a mesh: seq: 16 (over z, y, x), batch: 2 (over core).
Axes of the slice: x: 2, y: 2, z: 4, core: 2. Of those that a mesh axis runs over, the one named last changes fastest.
Arguments:
- inputs: bfloat16 [2, 2048, 2048], P('batch', 'seq'), may hold values from -6 to 6
- cotangent: bfloat16 [2, 2048, 1024], P('batch', 'seq'), may hold values from -48 to 48
- w_query: bfloat16 [2048, 128], replicated, may hold values from -0.125 to 0.125
- w_key: bfloat16 [2048, 128], replicated, may hold values from -0.125 to 0.125
- w_value: bfloat16 [2048, 1024], replicated, may hold values from -0.125 to 0.125
Outputs:
- grad_inputs: bfloat16 [2, 2048, 2048], P('batch', 'seq')
- grad_w_query: float32 [2048, 128], P(('seq', 'batch'))
- grad_w_key: float32 [2048, 128], P(('seq', 'batch'))
- grad_w_value: float32 [2048, 1024], P(('seq', 'batch'))
All inputs are finite; a program needn't handle non-finite values.
Results may differ from a plain program's by a relative error of at most 0.006.
Values sent between devices are 32-bit elements; how exact they have to be, the bound alone decides.
A program may use at most 128 MiB of HBM per device.

v0:
```python
import functools
import math

import jax
import jax.numpy as jnp
import numpy as np
from jax import lax
from jax.experimental import pallas as pl
from jax.experimental.pallas import tpu as pltpu
from jax.sharding import PartitionSpec as P

H = 8
DK = 16
DV = 128
AUX = 16
MESH = pl.DeviceIdType.MESH
BF = jnp.bfloat16
F32 = jnp.float32


def group(kind, outer, inner):
    seq = lax.axis_index("seq")
    core = lax.axis_index("batch")
    high = seq // inner
    low = seq % inner
    if kind == "seq":
        return outer * inner, seq, lambda j: (j, core)
    if kind == "plane":
        return inner * 2, low * 2 + core, lambda j: (high * inner + j // 2, j % 2)
    if kind == "line":
        return outer, high, lambda j: (j * inner + low, core)
    if kind == "chips":
        return inner, low, lambda j: (high * inner + j, core)
    return 2, core, lambda j: (seq, j)


def greet(groups):
    barrier = pltpu.get_barrier_semaphore()
    total = 0
    for size, me, where in groups:
        for k in range(1, size):
            pl.semaphore_signal(
                barrier, inc=1, device_id=where((me + k) % size), device_id_type=MESH
            )
        total += size - 1
    pl.semaphore_wait(barrier, total)


def push(src, dst, send, recv, device):
    copy = pltpu.make_async_remote_copy(
        src_ref=src,
        dst_ref=dst,
        send_sem=send,
        recv_sem=recv,
        device_id=device,
        device_id_type=MESH,
    )
    copy.start()
    return copy


VMEM = pl.BlockSpec(memory_space=pltpu.VMEM)
HBM = pl.BlockSpec(memory_space=pl.ANY)


def sems(*sizes):
    return pltpu.SemaphoreType.DMA(sizes)


def params(number):
    return pltpu.CompilerParams(
        collective_id=number, has_side_effects=True, vmem_limit_bytes=60 << 20
    )


def dot(left, right, dims):
    return lax.dot_general(left, right, ((dims[:1], dims[1:]), ((), ())), preferred_element_type=F32)


def halves(a):
    high = a.astype(BF)
    return high, (a - high.astype(F32)).astype(BF)


def dot2(pair, right, dims):
    return dot(pair[0], right, dims) + dot(pair[1], right, dims)


def dot2r(left, pair, dims):
    return dot(left, pair[0], dims) + dot(left, pair[1], dims)


def dot3(lefts, rights, dims):
    return (
        dot(lefts[0], rights[0], dims)
        + dot(lefts[0], rights[1], dims)
        + dot(lefts[1], rights[0], dims)
    )


def coefs():
    table = np.where(np.eye(DK) > 0, 1.0 / math.sqrt(2.0), 1.0).astype(np.float32)
    table = table * (np.arange(DK)[:, None] <= np.arange(DK)[None, :])
    half = DK // 2
    rows = np.concatenate([table[:half].reshape(-1), table[half:, half:].reshape(-1)])
    return np.ascontiguousarray(np.broadcast_to(rows[:, None], (rows.size, 128)))


def phi(u, coef):
    half = DK // 2
    lanes = u.shape[1]
    pieces = []
    for i in range(DK):
        low = u if i < half else u[half:]
        pieces.append(u[i : i + 1] * low)
    pairs = jnp.concatenate(pieces, 0) * coef
    first = (lax.broadcasted_iota(jnp.int32, (AUX, lanes), 0) == 0).astype(F32)
    return jnp.concatenate([pairs, u, first], 0)


def pull(u, grad, coef):
    half = DK // 2
    pairs = grad[: coef.shape[0]] * coef
    linear = grad[coef.shape[0] : coef.shape[0] + DK]
    rows = lax.broadcasted_iota(jnp.int32, u.shape, 0)
    total = linear
    lower = jnp.zeros_like(u[half:])
    at = 0
    for i in range(DK):
        if i < half:
            piece = pairs[at : at + DK]
            at += DK
            total = total + piece * u[i : i + 1]
            mine = jnp.sum(piece * u, 0, keepdims=True)
        else:
            piece = pairs[at : at + half]
            at += half
            lower = lower + piece * u[i : i + 1]
            mine = jnp.sum(piece * u[half:], 0, keepdims=True)
        total = total + jnp.where(rows == i, mine, 0.0)
    return total + jnp.concatenate([jnp.zeros_like(lower), lower], 0)


def attention_kernel(
    wide, outer, inner, r_ref, c_ref, x_ref, got_ref, xb_ref,
    o_ref, fq_ref, fk_ref, va_ref, ah, al, gh, gl, nh, nl, st_ref, gi_ref, pg_ref,
    send_i, recv_i, send_x, recv_x, send_q, recv_q, send_r, recv_r,
):
    blocks, _, tokens = r_ref.shape
    size, me, where = group("seq", outer, inner)
    chips, low, chip = group("chips", outer, inner)
    _, core, sibling = group("pair", outer, inner)
    rows = st_ref.shape[2] // outer
    for j in range(inner):
        for z in range(outer):
            at = (z * inner + j) * rows
            st_ref[j, :, z * rows : (z + 1) * rows] = x_ref[:, at : at + rows].astype(F32)
    greet([(size, me, where), (chips, low, chip), (2, core, sibling)])
    inside = []
    for k in range(1, chips):
        peer = (low + k) % chips
        inside.append(
            push(st_ref.at[peer], gi_ref.at[low], send_i.at[k], recv_i.at[k], chip(peer))
        )
    gi_ref[low] = st_ref[low]
    length = 2 * tokens
    chunks = blocks // 2
    feats = fq_ref.shape[1]
    coef = jnp.concatenate([c_ref[...]] * (length // 128), 1)
    causal = lax.broadcasted_iota(jnp.int32, (length, length), 0) <= lax.broadcasted_iota(
        jnp.int32, (length, length), 1
    )
    aux_row = lax.broadcasted_iota(jnp.int32, (AUX, length), 0) == 0

    def block(c):
        return jnp.concatenate([r_ref[2 * c], r_ref[2 * c + 1]], 1)

    def store(c, start, rows):
        size = rows.shape[0]
        o_ref[2 * c, start : start + size, :] = rows[:, :tokens]
        o_ref[2 * c + 1, start : start + size, :] = rows[:, tokens:]

    def forward(c, state):
        both = block(c)
        uq = both[:DK] * 0.5
        uk = both[DK : 2 * DK] * 0.5
        val = both[2 * DK : 2 * DK + wide]
        up = both[2 * DK + wide :]
        fq = phi(uq, coef).astype(BF)
        fk = phi(uk, coef).astype(BF)
        va = jnp.concatenate([val, aux_row.astype(F32)], 0).astype(BF)
        fq_ref[c] = fq
        fk_ref[c] = fk
        va_ref[c] = va
        attn = halves(jnp.where(causal, dot(fk, fq, (0, 0)), 0.0))
        ah[c] = attn[0]
        al[c] = attn[1]
        held = halves(state)
        top = dot2r(va, attn, (1, 0)) + dot2(held, fq, (1, 0))
        scale = 1.0 / top[wide : wide + 1]
        numer = up * scale
        denom = -jnp.sum(numer * top[:wide], 0, keepdims=True) * scale
        gn = halves(jnp.concatenate([numer, jnp.where(aux_row, denom, 0.0)], 0))
        nh[c] = gn[0]
        nl[c] = gn[1]
        ga = halves(jnp.where(causal, dot2r(va, gn, (0, 0)), 0.0))
        gh[c] = ga[0]
        gl[c] = ga[1]
        gfq = dot2r(fk, ga, (1, 0)) + dot3(held, gn, (0, 0))
        store(c, 0, pull(uq, gfq, coef) * 0.5)
        return state + dot(va, fk, (1, 1))

    zero = jnp.zeros((wide + AUX, feats), F32)
    lax.fori_loop(0, chunks, forward, zero)

    def give(start, count, send, recv):
        copies = []
        for k in range(1, size):
            peer = (me + k) % size
            src = o_ref.at[peer, pl.ds(start, count)]
            dst = got_ref.at[me, pl.ds(start, count)]
            copies.append(push(src, dst, send.at[k], recv.at[k], where(peer)))
        return copies

    returns = give(0, DK, send_q, recv_q)

    def backward(step, state):
        c = chunks - 1 - step
        uk = block(c)[DK : 2 * DK] * 0.5
        fq, fk, va = fq_ref[c], fk_ref[c], va_ref[c]
        attn = (ah[c], al[c])
        ga = (gh[c], gl[c])
        gn = (nh[c], nl[c])
        held = halves(state)
        gv = dot3(gn, attn, (1, 1)) + dot2(held, fk, (1, 0))
        store(c, 2 * DK, gv[:wide])
        gfk = dot2r(fq, ga, (1, 1)) + dot2(held, va, (0, 0))
        store(c, DK, pull(uk, gfk, coef) * 0.5)
        return state + dot2(gn, fq, (1, 1))

    lax.fori_loop(0, chunks, backward, zero)
    returns += give(DK, DK + wide, send_r, recv_r)
    got_ref[me] = o_ref[me]
    for copy in inside:
        copy.wait()
    pair = push(gi_ref, pg_ref, send_x.at[0], recv_x.at[0], sibling(1 - core))
    for j in range(inner):
        xb_ref[2 * j + core] = gi_ref[j].astype(BF)
    pair.wait()
    for j in range(inner):
        xb_ref[2 * j + 1 - core] = pg_ref[j].astype(BF)
    for copy in returns:
        copy.wait()


def attention(received, tokens_in, wide, outer, inner):
    blocks, _, tokens = received.shape
    coef = coefs()
    feats = coef.shape[0] + DK + AUX
    chunks, length = blocks // 2, 2 * tokens
    width = tokens_in.shape[1] // inner
    square = pltpu.VMEM((chunks, length, length), BF)
    grads = pltpu.VMEM((chunks, wide + AUX, length), BF)
    feat = pltpu.VMEM((chunks, feats, length), BF)
    result = (blocks, 2 * DK + wide, tokens)
    group_in = pltpu.VMEM((inner, tokens, width), F32)
    scratch = [pltpu.VMEM(result, F32), feat, feat, grads, square, square, square, square]
    scratch += [grads, grads, group_in, group_in, group_in]
    scratch += [sems(inner)] * 2 + [sems(1)] * 2 + [sems(blocks)] * 4
    return pl.pallas_call(
        functools.partial(attention_kernel, wide, outer, inner),
        out_shape=[
            jax.ShapeDtypeStruct(result, F32),
            jax.ShapeDtypeStruct((2 * inner, tokens, width), BF),
        ],
        in_specs=[VMEM] * 3,
        out_specs=[VMEM] * 2,
        scratch_shapes=scratch,
        compiler_params=params(1),
    )(received, jnp.asarray(coef), tokens_in)


def front_kernel(
    outer, inner, x_ref, c_ref, wq_hbm, wk_hbm, wv_hbm, out_ref,
    wq_ref, wk_ref, wv_ref, own_ref, up_ref, load, send_u, recv_u, send_p, recv_p,
):
    loads = []
    for n, (src, dst) in enumerate(((wq_hbm, wq_ref), (wk_hbm, wk_ref), (wv_hbm, wv_ref))):
        copy = pltpu.make_async_copy(src, dst, load.at[n])
        copy.start()
        loads.append(copy)
    size, me, where = group("seq", outer, inner)
    split = size // H
    wide = DV // split
    cut = 2 * DK + wide
    for h in range(H):
        flat = c_ref[:, h * DV : (h + 1) * DV].astype(F32).T
        for n in range(split):
            up_ref[h * split + n] = flat[n * wide : (n + 1) * wide]
    greet([(size, me, where)])
    copies = []
    for k in range(1, size):
        peer = (me + k) % size
        dst = out_ref.at[me, pl.ds(cut, wide)]
        copies.append(push(up_ref.at[peer], dst, send_u.at[k], recv_u.at[k], where(peer)))
    x = x_ref[...]
    for n, (w_ref, copy) in enumerate(zip((wq_ref, wk_ref), loads)):
        copy.wait()
        flat = dot(x, w_ref[...], (1, 0)).T
        for s in range(size):
            at = (s // split) * DK
            own_ref[s, n * DK : (n + 1) * DK, :] = flat[at : at + DK]
    loads[2].wait()
    for h in range(H):
        flat = dot(x, wv_ref[:, h * DV : (h + 1) * DV], (1, 0)).astype(BF).astype(F32).T
        for n in range(split):
            own_ref[h * split + n, 2 * DK :, :] = flat[n * wide : (n + 1) * wide]
    for k in range(1, size):
        peer = (me + k) % size
        dst = out_ref.at[me, pl.ds(0, cut)]
        copies.append(push(own_ref.at[peer], dst, send_p.at[k], recv_p.at[k], where(peer)))
    out_ref[me, :cut, :] = own_ref[me]
    out_ref[me, cut:, :] = up_ref[me]
    for copy in copies:
        copy.wait()


def front(tokens, upstream, weights, outer, inner):
    seqs = outer * inner
    length = tokens.shape[0]
    wide = DV * H // seqs
    cut = 2 * DK + wide
    scratch = [pltpu.VMEM(w.shape, w.dtype) for w in weights]
    scratch += [pltpu.VMEM((seqs, cut, length), F32), pltpu.VMEM((seqs, wide, length), F32)]
    return pl.pallas_call(
        functools.partial(front_kernel, outer, inner),
        out_shape=jax.ShapeDtypeStruct((seqs, cut + wide, length), F32),
        in_specs=[VMEM] * 2 + [HBM] * 3,
        out_specs=VMEM,
        scratch_shapes=scratch + [sems(3)] + [sems(seqs)] * 4,
        compiler_params=params(0),
    )(tokens, upstream, *weights)


def tail_kernel(
    outer, inner, pieces, g_ref, xb_ref, wq_hbm, wk_hbm, wv_hbm, gi_ref, o_ref,
    wq_ref, wk_ref, wv_ref, jt_ref, jb_ref, gj_ref, ls_ref, lr_ref, fs_ref, os_ref,
    load, send_j, recv_j, send_l, recv_l, send_o, recv_o,
):
    loads = []
    for n, (src, dst) in enumerate(((wq_hbm, wq_ref), (wk_hbm, wk_ref), (wv_hbm, wv_ref))):
        copy = pltpu.make_async_copy(src, dst, load.at[n])
        copy.start()
        loads.append(copy)
    plane, mine, where = group("plane", outer, inner)
    lines, high, along = group("line", outer, inner)
    _, core, sibling = group("pair", outer, inner)
    greet([(plane, mine, where), (lines, high, along), (2, core, sibling)])
    other = 1 - core
    seqs = outer * inner
    split = seqs // H
    wide = DV // split
    blocks = []
    for n in range(2):
        rows = []
        for h in range(H):
            total = g_ref[h * split, n * DK : (n + 1) * DK, :]
            for s in range(1, split):
                total = total + g_ref[h * split + s, n * DK : (n + 1) * DK, :]
            rows.append(total)
        blocks.append(jnp.concatenate(rows, 0))
    for h in range(H):
        blocks.append(
            jnp.concatenate([g_ref[h * split + s, 2 * DK :, :] for s in range(split)], 0)
        )
    for i in range(pieces):
        for half in range(2):
            jb_ref[half, i] = blocks[half * pieces + i].astype(BF).astype(F32)
    gathers = []
    for i in range(pieces):
        row = []
        for k in range(1, plane):
            peer = (mine + k) % plane
            src = jb_ref.at[peer % 2, i]
            row.append(
                push(src, gj_ref.at[i, mine], send_j.at[i, k], recv_j.at[i, k], where(peer))
            )
        gathers.append(row)
    for n, block in enumerate(blocks):
        jt_ref[:, n * DV : (n + 1) * DV] = block.T.astype(BF)
    for i in range(pieces):
        gj_ref[i, mine] = jb_ref[core, i]
    for copy in loads:
        copy.wait()
    depth = gi_ref.shape[1] // pieces // 256 * 256
    starts = [i * depth for i in range(pieces)] + [gi_ref.shape[1]]
    tokens = plane * xb_ref.shape[1]
    rows = xb_ref.shape[2] // lines
    reduces = []
    for i in range(pieces):
        cut = slice(starts[i], starts[i + 1])
        total = dot(jt_ref[:, :DV], wq_ref[cut, :], (1, 1))
        total = total + dot(jt_ref[:, DV : 2 * DV], wk_ref[cut, :], (1, 1))
        total = total + dot(jt_ref[:, 2 * DV :], wv_ref[cut, :], (1, 1))
        gi_ref[:, cut] = total.astype(BF)
        for copy in gathers[i]:
            copy.wait_recv()
        grads = jnp.concatenate([gj_ref[i, j].astype(BF) for j in range(plane)], 1)
        part = dot(grads, xb_ref[...].reshape(tokens, xb_ref.shape[2]), (1, 0))
        for z in range(lines):
            ls_ref[i, z] = part[:, z * rows : (z + 1) * rows]
        row = []
        for k in range(1, lines):
            peer = (high + k) % lines
            row.append(
                push(ls_ref.at[i, peer], lr_ref.at[i, k], send_l.at[i, k], recv_l.at[i, k], along(peer))
            )
        reduces.append(row)
    lasts = []
    keep = rows // 2
    for i in range(pieces):
        total = ls_ref[i, high]
        for k, copy in enumerate(reduces[i]):
            copy.wait_recv()
            total = total + lr_ref[i, k + 1]
        fs_ref[i] = total.T
        src = fs_ref.at[i, pl.ds(pl.multiple_of(other * keep, keep), keep)]
        lasts.append(push(src, os_ref.at[i], send_o.at[i], recv_o.at[i], sibling(other)))
        o_ref[core * pieces + i] = fs_ref[i, pl.ds(pl.multiple_of(core * keep, keep), keep), :]
    for i, copy in enumerate(lasts):
        copy.wait_recv()
        o_ref[other * pieces + i] = os_ref[i]
    for row in gathers + reduces + [lasts]:
        for copy in row:
            copy.wait_send()


def tail(grads, inside, weights, outer, inner):
    seqs, _, length = grads.shape
    width = weights[0].shape[0]
    pieces = sum(w.shape[1] for w in weights) // (2 * DV)
    rows = width // seqs
    plane = 2 * inner
    vm = lambda *shape: pltpu.VMEM(shape, F32)
    scratch = [pltpu.VMEM(w.shape, w.dtype) for w in weights] + [
        pltpu.VMEM((length, 2 * pieces * DV), BF),
        vm(2, pieces, DV, length),
        vm(pieces, plane, DV, length),
        vm(pieces, outer, DV, rows),
        vm(pieces, outer, DV, rows),
        vm(pieces, rows, DV),
        vm(pieces, rows // 2, DV),
        sems(3),
        sems(pieces, plane), sems(pieces, plane),
        sems(pieces, outer), sems(pieces, outer),
        sems(pieces), sems(pieces),
    ]
    return pl.pallas_call(
        functools.partial(tail_kernel, outer, inner, pieces),
        out_shape=[
            jax.ShapeDtypeStruct((length, width), BF),
            jax.ShapeDtypeStruct((2 * pieces, rows // 2, DV), F32),
        ],
        in_specs=[VMEM] * 2 + [HBM] * 3,
        out_specs=[VMEM] * 2,
        scratch_shapes=scratch,
        compiler_params=params(2),
    )(grads, inside, *weights)


def finish_kernel(gi_ref, o_ref, in_ref, oq_ref, ok_ref, ov_ref):
    in_ref[0] = gi_ref[...]
    oq_ref[...] = o_ref[0]
    ok_ref[...] = o_ref[1]
    for n in range(H):
        ov_ref[:, n * DV : (n + 1) * DV] = o_ref[2 + n]


def finish(grad_in, blocks):
    _, rows, lanes = blocks.shape
    return pl.pallas_call(
        finish_kernel,
        out_shape=[
            jax.ShapeDtypeStruct((1,) + grad_in.shape, BF),
            jax.ShapeDtypeStruct((rows, lanes), F32),
            jax.ShapeDtypeStruct((rows, lanes), F32),
            jax.ShapeDtypeStruct((rows, H * lanes), F32),
        ],
        in_specs=[VMEM] * 2,
        out_specs=[VMEM] * 4,
    )(grad_in, blocks)


def body(inputs, cotangent, w_query, w_key, w_value):
    seqs = lax.axis_size("seq")
    outer = 4 if seqs % 4 == 0 else 1
    inner = seqs // outer
    wide = DV * H // seqs
    tokens = inputs[0]
    weights = (w_query, w_key, w_value)
    received = front(tokens, cotangent[0], weights, outer, inner)
    grads, inside = attention(received, tokens, wide, outer, inner)
    return tuple(finish(*tail(grads, inside, weights, outer, inner)))


def solution(mesh):
    in_specs = (P("batch", "seq", None), P("batch", "seq", None), P(), P(), P())
    out_specs = (
        P("batch", "seq", None),
        P(("seq", "batch"), None),
        P(("seq", "batch"), None),
        P(("seq", "batch"), None),
    )
    return jax.shard_map(body, mesh=mesh, in_specs=in_specs, out_specs=out_specs, check_vma=False)
```

profile of v0, /device:TPU:0, one launch (start us, length us, event | category | flops | bytes accessed | tf_op | source)
XLA Modules:
  0.0 120.8 jit_solution(6320827708486719574)
XLA Ops:
  0.6 32.6 %shard_map.93.r_ref = f32[16,160,128]{2,1,0:T(8,128)} custom-call(bf16[128,2048]{1,0:T(8,128)(2,1)} %bitcast.2, bf16[128,1024]{1,0:T(8,128)(2,1)} %bitcast.4, bf16[2048,128]{1,0:T(8,128)(2,1)} %wq_hbm.3, bf16[2048,128]{1,0:T(8,128)(2,1)} %wk_hbm.3, bf16[2048,1024]{1,0:T(8,128)(2,1)} %wv_hbm.3), custom_call_target="tpu_custom_call" | custom-call | tf_op jit(solution)/shard_map/pallas_call | solution.py:335
  33.3 37.2 %shard_map.94 = (f32[16,96,128]{2,1,0:T(8,128)}, bf16[8,128,512]{2,1,0:T(8,128)(2,1)}) custom-call(f32[16,160,128]{2,1,0:T(8,128)} %shard_map.93.r_ref, f32[192,128]{1,0:T(8,128)} %constant.2.clone.c_ref, bf16[128,2048]{1,0:T(8,128)(2,1)} %bitcast.3), custom_call_target="tpu_custom_call" | custom-call | tf_op jit(solution)/shard_map/pallas_call | solution.py:270
  70.5 48.2 %shard_map.95 = (bf16[128,2048]{1,0:T(8,128)(2,1)}, f32[10,64,128]{2,1,0:T(8,128)}) custom-call(f32[16,96,128]{2,1,0:T(8,128)} %get-tuple-element.8.g_ref, bf16[8,128,512]{2,1,0:T(8,128)(2,1)} %get-tuple-element.9.xb_ref, bf16[2048,128]{1,0:T(8,128)(2,1)} %wq_hbm.3, bf16[2048,128]{1,0:T(8,128)(2,1)} %wk_hbm.3, bf16[2048,1024]{1,0:T(8,128)(2,1)} %wv_hbm.3), custom_call_target="tpu_custom_call" | custom-call | tf_op jit(solution)/shard_map/pallas_call | solution.py:458
  118.7 2.1 %shard_map.96 = (bf16[1,128,2048]{2,1,0:T(8,128)(2,1)}, f32[64,128]{1,0:T(8,128)}, f32[64,128]{1,0:T(8,128)}, f32[64,1024]{1,0:T(8,128)}) custom-call(bf16[128,2048]{1,0:T(8,128)(2,1)} %get-tuple-element.10.gi_ref, f32[10,64,128]{2,1,0:T(8,128)} %get-tuple-element.11.o_ref), custom_call_target="tpu_custom_call" | custom-call | tf_op jit(solution)/shard_map/pallas_call | solution.py:481
where the time goes:
time: 121 us
  Pallas kernels  120 us (99%)
    pallas_call x1, Pallas kernels, tail(): pl.pallas_call(functools.partial(tail_kernel, outer, inner, pieces), out_...  48.2 us
    pallas_call x1, Pallas kernels, attention(): pl.pallas_call(functools.partial(attention_kernel, wide, outer, inner), o...  37.2 us
    pallas_call x1, Pallas kernels, front(): pl.pallas_call(functools.partial(front_kernel, outer, inner), out_shape=j...  32.6 us

commit v1 on v0

v1 whole, which is shorter than its diff:
```python
import functools
import math

import jax
import jax.numpy as jnp
from jax import lax
from jax.experimental import pallas as pl
from jax.experimental.pallas import tpu as pltpu
from jax.sharding import PartitionSpec as P

H = 8
DK = 16
DV = 128
AUX = 16
PAIRS = DK * (DK + 1) // 2
FEATS = PAIRS + DK + 8
HALF = DK + DV // 2
PIECES = 2
ROWS = HALF // PIECES
BITS = (1, 2, 4)
MESH = pl.DeviceIdType.MESH
BF = jnp.bfloat16
F32 = jnp.float32
VMEM = pl.BlockSpec(memory_space=pltpu.VMEM)
HBM = pl.BlockSpec(memory_space=pl.ANY)


def push(src, dst, send, recv, device):
    copy = pltpu.make_async_remote_copy(
        src_ref=src,
        dst_ref=dst,
        send_sem=send,
        recv_sem=recv,
        device_id=device,
        device_id_type=MESH,
    )
    copy.start()
    return copy


def sems(*sizes):
    return pltpu.SemaphoreType.DMA(sizes)


def dot(left, right, dims):
    return lax.dot_general(left, right, ((dims[:1], dims[1:]), ((), ())), preferred_element_type=F32)


def halves(a):
    high = a.astype(BF)
    return high, (a - high.astype(F32)).astype(BF)


def dot2(pair, right, dims):
    return dot(pair[0], right, dims) + dot(pair[1], right, dims)


def dot2r(left, pair, dims):
    return dot(left, pair[0], dims) + dot(left, pair[1], dims)


def dot3(lefts, rights, dims):
    return (
        dot(lefts[0], rights[0], dims)
        + dot(lefts[0], rights[1], dims)
        + dot(lefts[1], rights[0], dims)
    )


def flip(rank, mask):
    for bit in BITS:
        if mask & bit:
            rank = rank + bit - 2 * bit * ((rank // bit) % 2)
    return rank


def phi(u):
    half = DK // 2
    lanes = u.shape[1]
    pieces = [u * u * math.sqrt(0.5)]
    for s in range(1, half):
        pieces.append(u * pltpu.roll(u, DK - s, 0))
    pieces.append(u[:half] * u[half:])
    pieces.append(u)
    pieces.append((lax.broadcasted_iota(jnp.int32, (8, lanes), 0) == 0).astype(F32))
    return jnp.concatenate(pieces, 0)


def pull(u, grad):
    half = DK // 2
    total = grad[PAIRS : PAIRS + DK] + grad[:DK] * u * math.sqrt(2.0)
    for s in range(1, half):
        piece = grad[s * DK : (s + 1) * DK]
        total = total + piece * pltpu.roll(u, DK - s, 0) + pltpu.roll(piece * u, s, 0)
    last = grad[half * DK : half * DK + half]
    return total + jnp.concatenate([last * u[half:], last * u[:half]], 0)


def pack(values, norms):
    low = norms[:8, :DV]
    high = jnp.concatenate([norms[:8, DV:], jnp.zeros((8, 2 * DV - FEATS), F32)], 1)
    return jnp.concatenate([values, low, high], 0)


def unpack(packed):
    values = packed[:FEATS]
    norms = jnp.concatenate([packed[FEATS : FEATS + 8], packed[FEATS + 8 :, : FEATS - DV]], 1)
    return values, jnp.concatenate([norms, jnp.zeros((AUX - 8, FEATS), F32)], 0)


def fused_kernel(
    ng, x_hbm, c_hbm, wq_hbm, wk_hbm, wv_hbm, gi_ref, out_ref,
    x_ref, c_ref, wq_ref, wk_ref, wv_ref, own, rec, st, xg, xp, xb,
    fqs, fks, vas, ah, al, nh, nl, tops, pv, rv, gvs, gfks,
    ssend, srecv, rsend, rrecv, o, gj, ls, lr, ret, jt, f2, fs,
    load, us, ur, qs, qr, xs, xr, ps, pr, ss, sr, rs, rr, gs, gr, ts, tr, bs, br, ds, dr,
):
    seq = lax.axis_index("seq")
    core = lax.axis_index("batch")
    other = 1 - core
    g = seq // H
    r = seq % H
    anti = H - 1 - r
    length = x_ref.shape[0]
    width = x_ref.shape[1]
    owned = width // (ng * H)
    slots = 2 * ng
    chunks = H // 2
    span = 2 * length

    def mate(k):
        return (g * H + flip(r, k), core)

    loads = []
    for n, (src, dst) in enumerate(
        ((c_hbm, c_ref), (x_hbm, x_ref), (wq_hbm, wq_ref), (wk_hbm, wk_ref), (wv_hbm, wv_ref))
    ):
        copy = pltpu.make_async_copy(src, dst, load.at[n])
        copy.start()
        loads.append(copy)

    peers = [mate(k) for k in range(1, H)] + [(seq, other)]
    peers += [(g * H + flip(r, bit), other) for bit in BITS]
    for d in range(1, ng):
        far = (g + d) % ng
        peers += [(far * H + r, core), (far * H + anti, core)]
    barrier = pltpu.get_barrier_semaphore()
    for peer in peers:
        pl.semaphore_signal(barrier, inc=1, device_id=peer, device_id_type=MESH)

    everything = []
    cut = 2 * DK + DV
    loads[0].wait()
    for h in range(H):
        own[h, cut:, :] = c_ref[:, h * DV : (h + 1) * DV].astype(F32).T
    pl.semaphore_wait(barrier, len(peers))
    ups = []
    for k in range(1, H):
        src = own.at[flip(r, k), pl.ds(cut, DV)]
        ups.append(push(src, rec.at[r, pl.ds(cut, DV)], us.at[k], ur.at[k], mate(k)))
    loads[1].wait()
    x = x_ref[...]
    for n, w_ref in enumerate((wq_ref, wk_ref)):
        loads[2 + n].wait()
        flat = dot(x, w_ref[...], (1, 0)).T
        for h in range(H):
            own[h, n * DK : (n + 1) * DK, :] = flat[h * DK : (h + 1) * DK]
    loads[4].wait()
    for h in range(H):
        own[h, 2 * DK : cut, :] = dot(x, wv_ref[:, h * DV : (h + 1) * DV], (1, 0)).T
    qkv = []
    for k in range(1, H):
        src = own.at[flip(r, k), pl.ds(0, cut)]
        qkv.append(push(src, rec.at[r, pl.ds(0, cut)], qs.at[k], qr.at[k], mate(k)))
    rec[r] = own[r]

    for cls in range(H // 2):
        for a in range(slots):
            at = ((a // 2) * H + (cls if a % 2 == 0 else H - 1 - cls)) * owned
            st[cls, :, a * owned : (a + 1) * owned] = x_ref[:, at : at + owned].astype(F32)

    def kind(rank):
        return rank + (rank // 4) * (H - 1 - 2 * rank)

    def exchange(ks):
        return [
            push(st.at[kind(flip(r, k))], xg.at[r], xs.at[k], xr.at[k], mate(k)) for k in ks
        ]

    shares = exchange((1, 2, 3))
    xg[r] = st[kind(r)]

    causal = lax.broadcasted_iota(jnp.int32, (span, span), 0) <= lax.broadcasted_iota(
        jnp.int32, (span, span), 1
    )
    ones = (lax.broadcasted_iota(jnp.int32, (AUX, span), 0) == 0).astype(F32)
    first = lax.broadcasted_iota(jnp.int32, (AUX, span), 0) == 0

    def part(c, start, count):
        rows = slice(start, start + count)
        return jnp.concatenate([rec[2 * c, rows, :], rec[2 * c + 1, rows, :]], 1)

    for copy in ups + qkv:
        copy.wait_recv()

    values = jnp.zeros((FEATS, DV), F32)
    norms = jnp.zeros((AUX, FEATS), F32)
    norm_at = []
    for c in range(chunks):
        fq = phi(part(c, 0, DK) * 0.5).astype(BF)
        fk = phi(part(c, DK, DK) * 0.5).astype(BF)
        va = jnp.concatenate([part(c, 2 * DK, DV), ones], 0).astype(BF)
        fqs[c] = fq
        fks[c] = fk
        vas[c] = va
        pv[c] = values
        norm_at.append(norms)
        values = values + dot(fk, va[:DV], (1, 1))
        norms = norms + dot(va[DV:], fk, (1, 1))
    ssend[...] = pack(values, norms)
    states = []
    for d in range(1, ng):
        to = (((g + d) % ng) * H + r, core)
        states.append(push(ssend, srecv.at[d], ss.at[d], sr.at[d], to))
    shares += exchange((4, 5))

    for c in range(chunks):
        fq, fk, va = fqs[c], fks[c], vas[c]
        attn = halves(jnp.where(causal, dot(fk, fq, (0, 0)), 0.0))
        ah[c] = attn[0]
        al[c] = attn[1]
        top = dot2r(va, attn, (1, 0))
        if c > 0:
            top = top + jnp.concatenate(
                [dot2(halves(pv[c]), fq, (0, 0)), dot2(halves(norm_at[c]), fq, (1, 0))], 0
            )
        tops[c] = top

    packed = jnp.zeros(ssend.shape, F32)
    for d, copy in enumerate(states, 1):
        copy.wait_recv()
        packed = packed + jnp.where((g - d + ng) % ng < g, srecv[d], 0.0)
    in_values, in_norms = unpack(packed)
    in_pair, in_norm_pair = halves(in_values), halves(in_norms)

    back = jnp.zeros((FEATS, DV), F32)
    back_norm = jnp.zeros((AUX, FEATS), F32)
    back_norm_at = [None] * chunks
    for c in reversed(range(chunks)):
        fq = fqs[c]
        top = tops[c] + jnp.concatenate(
            [dot2(in_pair, fq, (0, 0)), dot2(in_norm_pair, fq, (1, 0))], 0
        )
        scale = 1.0 / top[DV : DV + 1]
        numer = part(c, cut, DV) * scale
        denom = -jnp.sum(numer * top[:DV], 0, keepdims=True) * scale
        gn = halves(jnp.concatenate([numer, jnp.where(first, denom, 0.0)], 0))
        nh[c] = gn[0]
        nl[c] = gn[1]
        rv[c] = back
        back_norm_at[c] = back_norm
        back = back + dot2r(fq, (gn[0][:DV], gn[1][:DV]), (1, 1))
        back_norm = back_norm + dot2((gn[0][DV:], gn[1][DV:]), fq, (1, 1))
    rsend[...] = pack(back, back_norm)
    backs = []
    for d in range(1, ng):
        to = (((g + d) % ng) * H + r, core)
        backs.append(push(rsend, rrecv.at[d], rs.at[d], rr.at[d], to))
    shares += exchange((6, 7))

    def store(c, start, rows):
        half = 0 if start < HALF else 1
        at = start - half * HALF
        for b in range(2):
            o[2 * c + b, half, at : at + rows.shape[0], :] = rows[:, b * length : (b + 1) * length]

    for c in range(chunks):
        fq, fk, va = fqs[c], fks[c], vas[c]
        attn = (ah[c], al[c])
        gn = (nh[c], nl[c])
        ga = halves(jnp.where(causal, dot2r(va, gn, (0, 0)), 0.0))
        held = halves(pv[c] + in_values)
        held_norm = halves(norm_at[c] + in_norms)
        gfq = dot2r(fk, ga, (1, 0))
        gfq = gfq + dot3(held, (gn[0][:DV], gn[1][:DV]), (1, 0))
        gfq = gfq + dot3(held_norm, (gn[0][DV:], gn[1][DV:]), (0, 0))
        store(c, 0, pull(part(c, 0, DK) * 0.5, gfq) * 0.5)
        gv = dot3((gn[0][:DV], gn[1][:DV]), attn, (1, 1))
        gfk = dot2r(fq, ga, (1, 1))
        if c < chunks - 1:
            after = halves(rv[c])
            gv = gv + dot2(after, fk, (0, 0))
            gfk = gfk + dot2(after, va[:DV], (1, 0))
            gfk = gfk + dot2(halves(back_norm_at[c]), va[DV:], (0, 0))
        gvs[c] = gv
        gfks[c] = gfk

    base = (r // 4) * 4
    for copy in shares[:3]:
        copy.wait_recv()
    pairs = [push(xg.at[pl.ds(base, 4)], xp.at[pl.ds(base, 4)], ps.at[0], pr.at[0], (seq, other))]

    packed = jnp.zeros(rsend.shape, F32)
    for d, copy in enumerate(backs, 1):
        copy.wait_recv()
        packed = packed + jnp.where((g - d + ng) % ng > g, rrecv[d], 0.0)
    in_values, in_norms = unpack(packed)
    in_pair, in_norm_pair = halves(in_values), halves(in_norms)
    for c in range(chunks):
        fk, va = fks[c], vas[c]
        gv = gvs[c] + dot2(in_pair, fk, (0, 0))
        gfk = gfks[c] + dot2(in_pair, va[:DV], (1, 0)) + dot2(in_norm_pair, va[DV:], (0, 0))
        store(c, DK, gv[: DV // 2])
        store(c, HALF + DK, gv[DV // 2 :])
        store(c, HALF, pull(part(c, DK, DK) * 0.5, gfk) * 0.5)

    gathers = []
    for i in range(PIECES):
        row = []
        for n, bit in enumerate(BITS, 1):
            for half in range(2):
                row.append(
                    push(
                        o.at[:, half, pl.ds(i * ROWS, ROWS)],
                        gj.at[i, n, core],
                        gs.at[i, n, half],
                        gr.at[i, n, core],
                        (g * H + flip(r, bit), half),
                    )
                )
        row.append(
            push(
                o.at[:, other, pl.ds(i * ROWS, ROWS)],
                gj.at[i, 0, core],
                gs.at[i, 0, 0],
                gr.at[i, 0, core],
                (seq, other),
            )
        )
        gathers.append(row)
    returns = []
    for k in range(1, H):
        returns.append(push(o.at[flip(r, k)], ret.at[r], ts.at[k], tr.at[k], mate(k)))
    ret[r] = o[r]
    for i in range(PIECES):
        gj[i, 0, core] = o[:, core, i * ROWS : (i + 1) * ROWS, :]

    for copy in shares[3:]:
        copy.wait_recv()
    far = 4 - base
    pairs.append(push(xg.at[pl.ds(far, 4)], xp.at[pl.ds(far, 4)], ps.at[1], pr.at[1], (seq, other)))
    for j in range(H):
        xb[core, j * length : (j + 1) * length, :] = xg[j].astype(BF)
    for copy in pairs:
        copy.wait_recv()
    for j in range(H):
        xb[other, j * length : (j + 1) * length, :] = xp[j].astype(BF)

    def arrive(i, n, b):
        return pltpu.make_async_copy(gj.at[i, n, b], gj.at[i, n, b], gr.at[i, n, b])

    tokens = 2 * H * length
    sent = []
    for i in range(PIECES):
        for n in range(1, 1 + len(BITS)):
            for b in range(2):
                arrive(i, n, b).wait()
        arrive(i, 0, other).wait()
        rows = []
        for n in range(1 + len(BITS)):
            rows.append(
                jnp.concatenate([gj[i, n, b, j] for b in range(2) for j in range(H)], 1)
            )
        grads = jnp.concatenate(rows, 0).astype(BF)
        product = dot(grads, xb[...].reshape(tokens, slots * owned), (1, 0))
        for a in range(slots):
            ls[i, a] = product[:, a * owned : (a + 1) * owned]
        row = []
        for d in range(ng):
            for w in range(2):
                if d == 0 and w == 0:
                    continue
                group = (g + d) % ng
                rank = r if w == 0 else anti
                slot = group * 2 + rank // 4
                row.append(
                    push(
                        ls.at[i, slot], lr.at[i, d, w], bs.at[i, d, w], br.at[i, d, w],
                        (group * H + rank, core),
                    )
                )
        sent.append(row)

    for copy in returns:
        copy.wait_recv()
    blocks = []
    for n in range(2):
        blocks.append(jnp.concatenate([ret[h, n, :DK, :] for h in range(H)], 0))
    for h in range(H):
        blocks.append(jnp.concatenate([ret[h, 0, DK:, :], ret[h, 1, DK:, :]], 0))
    for n, block in enumerate(blocks):
        jt[:, n * DV : (n + 1) * DV] = block.T.astype(BF)
    step = 512
    for at in range(0, width, step):
        rows = slice(at, at + step)
        total = dot(jt[:, :DV], wq_ref[rows, :], (1, 1))
        total = total + dot(jt[:, DV : 2 * DV], wk_ref[rows, :], (1, 1))
        total = total + dot(jt[:, 2 * DV :], wv_ref[rows, :], (1, 1))
        gi_ref[:, rows] = total.astype(BF)

    swaps = []
    for i in range(PIECES):
        for copy in sent[i]:
            copy.wait_recv()
        mine = ls[i, g * 2 + r // 4]
        rest = lr[i, 0, 1]
        for d in range(1, ng):
            mine = mine + lr[i, d, 0]
            rest = rest + lr[i, d, 1]
        for n, bit in enumerate((0,) + BITS):
            f2[core, i, flip(r, bit)] = mine[n * ROWS : (n + 1) * ROWS]
            f2[core, i, flip(anti, bit)] = rest[n * ROWS : (n + 1) * ROWS]
        swaps.append(
            push(f2.at[core, i], f2.at[core, i], ds.at[i], dr.at[i], (seq, other))
        )
    for copy in swaps:
        copy.wait_recv()
    final = []
    for n in range(2):
        final.append(jnp.concatenate([f2[n, 0, h, :DK] for h in range(H)], 0))
    for h in range(H):
        parts = []
        for n in range(2):
            for i in range(PIECES):
                parts.append(f2[n, i, h, DK if i == 0 else 0 :])
        final.append(jnp.concatenate(parts, 0))
    keep = owned // 2
    for n, block in enumerate(final):
        fs[n] = block.T
        out_ref[n] = fs[n, pl.ds(pl.multiple_of(core * keep, keep), keep), :]
    everything += ups + qkv + shares + states + backs + pairs + returns + swaps
    for row in gathers + sent:
        everything += row
    for copy in everything:
        copy.wait_send()


def fused(tokens, upstream, weights, ng):
    length, width = tokens.shape
    owned = width // (ng * H)
    slots = 2 * ng
    chunks, span = H // 2, 2 * length
    vm = lambda *shape: pltpu.VMEM(shape, F32)
    half = lambda *shape: pltpu.VMEM(shape, BF)
    nb = 1 + len(BITS)
    scratch = [half(length, width), half(length, H * DV)]
    scratch += [pltpu.VMEM(w.shape, w.dtype) for w in weights]
    scratch += [
        vm(H, 2 * DK + 2 * DV, length), vm(H, 2 * DK + 2 * DV, length),
        vm(H // 2, length, slots * owned), vm(H, length, slots * owned),
        vm(H, length, slots * owned), half(2, H * length, slots * owned),
        half(chunks, FEATS, span), half(chunks, FEATS, span), half(chunks, DV + AUX, span),
        half(chunks, span, span), half(chunks, span, span),
        half(chunks, DV + AUX, span), half(chunks, DV + AUX, span),
        vm(chunks, DV + AUX, span), vm(chunks, FEATS, DV), vm(chunks, FEATS, DV),
        vm(chunks, DV, span), vm(chunks, FEATS, span),
        vm(FEATS + 16, DV), vm(ng, FEATS + 16, DV), vm(FEATS + 16, DV), vm(ng, FEATS + 16, DV),
        vm(H, 2, HALF, length), vm(PIECES, nb, 2, H, ROWS, length),
        vm(PIECES, slots, nb * ROWS, owned), vm(PIECES, ng, 2, nb * ROWS, owned),
        vm(H, 2, HALF, length), half(length, H * DV + 2 * DV),
        vm(2, PIECES, H, ROWS, owned), vm(2 + H, owned, DV),
        sems(5),
        sems(H), sems(H), sems(H), sems(H), sems(H), sems(H), sems(2), sems(2),
        sems(ng), sems(ng), sems(ng), sems(ng),
        sems(PIECES, nb, 2), sems(PIECES, nb, 2), sems(H), sems(H),
        sems(PIECES, ng, 2), sems(PIECES, ng, 2), sems(PIECES), sems(PIECES),
    ]
    return pl.pallas_call(
        functools.partial(fused_kernel, ng),
        out_shape=[
            jax.ShapeDtypeStruct((length, width), BF),
            jax.ShapeDtypeStruct((2 + H, owned // 2, DV), F32),
        ],
        in_specs=[HBM] * 5,
        out_specs=[VMEM] * 2,
        scratch_shapes=scratch,
        compiler_params=pltpu.CompilerParams(
            collective_id=0, has_side_effects=True, vmem_limit_bytes=60 << 20
        ),
    )(tokens, upstream, *weights)


def finish_kernel(gi_ref, o_ref, in_ref, oq_ref, ok_ref, ov_ref):
    in_ref[0] = gi_ref[...]
    oq_ref[...] = o_ref[0]
    ok_ref[...] = o_ref[1]
    for n in range(H):
        ov_ref[:, n * DV : (n + 1) * DV] = o_ref[2 + n]


def finish(grad_in, blocks):
    _, rows, lanes = blocks.shape
    return pl.pallas_call(
        finish_kernel,
        out_shape=[
            jax.ShapeDtypeStruct((1,) + grad_in.shape, BF),
            jax.ShapeDtypeStruct((rows, lanes), F32),
            jax.ShapeDtypeStruct((rows, lanes), F32),
            jax.ShapeDtypeStruct((rows, H * lanes), F32),
        ],
        in_specs=[VMEM] * 2,
        out_specs=[VMEM] * 4,
    )(grad_in, blocks)


def body(inputs, cotangent, w_query, w_key, w_value):
    ng = lax.axis_size("seq") // H
    weights = (w_query, w_key, w_value)
    return tuple(finish(*fused(inputs[0], cotangent[0], weights, ng)))


def solution(mesh):
    in_specs = (P("batch", "seq", None), P("batch", "seq", None), P(), P(), P())
    out_specs = (
        P("batch", "seq", None),
        P(("seq", "batch"), None),
        P(("seq", "batch"), None),
        P(("seq", "batch"), None),
    )
    return jax.shard_map(body, mesh=mesh, in_specs=in_specs, out_specs=out_specs, check_vma=False)
```

time: 121 us -> 89 us (0.74)
  Pallas kernels: 120 us -> 88 us
    pallas_call x3 -> x1, Pallas kernels: 118 us -> 86 us  [fused(): pl.pallas_call(functools.partial(fused_kernel, ng), out_shape=[jax.ShapeD...]
where the time goes in v1:
time: 89 us; the launch traced here: 88.6 us
  Pallas kernels  88 us (99%)
    pallas_call x1, Pallas kernels, fused(): pl.pallas_call(functools.partial(fused_kernel, ng), out_shape=[jax.ShapeD...  86 us
    pallas_call x1, Pallas kernels, finish(): pl.pallas_call(finish_kernel, out_shape=[jax.ShapeDtypeStruct((1,) + grad...  2.06 us

profile of v1, /device:TPU:0, one launch (start us, length us, event | category | flops | bytes accessed | tf_op | source)
XLA Modules:
  0.0 88.6 jit_solution(3545916856826981208)
XLA Ops:
  0.6 86.0 %shard_map.84 = (bf16[128,2048]{1,0:T(8,128)(2,1)}, f32[10,64,128]{2,1,0:T(8,128)}) custom-call(bf16[128,2048]{1,0:T(8,128)(2,1)} %bitcast.2, bf16[128,1024]{1,0:T(8,128)(2,1)} %bitcast.3, bf16[2048,128]{1,0:T(8,128)(2,1)} %wq_hbm.1, bf16[2048,128]{1,0:T(8,128)(2,1)} %wk_hbm.1, bf16[2048,1024]{1,0:T(8,128)(2,1)} %wv_hbm.1), custom_call_target="tpu_custom_call" | custom-call | tf_op jit(solution)/shard_map/pallas_call | solution.py:478
  86.6 2.1 %shard_map.85 = (bf16[1,128,2048]{2,1,0:T(8,128)(2,1)}, f32[64,128]{1,0:T(8,128)}, f32[64,128]{1,0:T(8,128)}, f32[64,1024]{1,0:T(8,128)}) custom-call(bf16[128,2048]{1,0:T(8,128)(2,1)} %get-tuple-element.6.gi_ref, f32[10,64,128]{2,1,0:T(8,128)} %get-tuple-element.7.o_ref), custom_call_target="tpu_custom_call" | custom-call | tf_op jit(solution)/shard_map/pallas_call | solution.py:503

commit v2 on v1

--- a/solution.py
+++ b/solution.py
@@ -15,9 +15,10 @@
 PAIRS = DK * (DK + 1) // 2
 FEATS = PAIRS + DK + 8
 HALF = DK + DV // 2
-PIECES = 2
+PIECES = 5
 ROWS = HALF // PIECES
 BITS = (1, 2, 4)
+PLANE = 4
 MESH = pl.DeviceIdType.MESH
 BF = jnp.bfloat16
 F32 = jnp.float32
@@ -112,15 +113,16 @@
     ng, x_hbm, c_hbm, wq_hbm, wk_hbm, wv_hbm, gi_ref, out_ref,
     x_ref, c_ref, wq_ref, wk_ref, wv_ref, own, rec, st, xg, xp, xb,
     fqs, fks, vas, ah, al, nh, nl, tops, pv, rv, gvs, gfks,
-    ssend, srecv, rsend, rrecv, o, gj, ls, lr, ret, jt, f2, fs,
-    load, us, ur, qs, qr, xs, xr, ps, pr, ss, sr, rs, rr, gs, gr, ts, tr, bs, br, ds, dr,
+    ssend, srecv, sin, rsend, rrecv, rin, o, gj, ls, lr, rt, jt, f2, fs,
+    load, us, ur, qs, qr, xs, xr, zs, zr, ps, pr, ss, sr, rs, rr,
+    gs, gr, hs, ts, tr, bs, br, ds, dr,
 ):
     seq = lax.axis_index("seq")
     core = lax.axis_index("batch")
     other = 1 - core
     g = seq // H
     r = seq % H
-    anti = H - 1 - r
+    mirror = flip(r, PLANE)
     length = x_ref.shape[0]
     width = x_ref.shape[1]
     owned = width // (ng * H)
@@ -143,12 +145,11 @@
     peers += [(g * H + flip(r, bit), other) for bit in BITS]
     for d in range(1, ng):
         far = (g + d) % ng
-        peers += [(far * H + r, core), (far * H + anti, core)]
+        peers += [(far * H + r, core), (far * H + mirror, core)]
     barrier = pltpu.get_barrier_semaphore()
     for peer in peers:
         pl.semaphore_signal(barrier, inc=1, device_id=peer, device_id_type=MESH)
 
-    everything = []
     cut = 2 * DK + DV
     loads[0].wait()
     for h in range(H):
@@ -174,21 +175,19 @@
         qkv.append(push(src, rec.at[r, pl.ds(0, cut)], qs.at[k], qr.at[k], mate(k)))
     rec[r] = own[r]
 
-    for cls in range(H // 2):
+    for cls in range(PLANE):
         for a in range(slots):
-            at = ((a // 2) * H + (cls if a % 2 == 0 else H - 1 - cls)) * owned
+            at = ((a // 2) * H + cls + PLANE * (a % 2)) * owned
             st[cls, :, a * owned : (a + 1) * owned] = x_ref[:, at : at + owned].astype(F32)
-
-    def kind(rank):
-        return rank + (rank // 4) * (H - 1 - 2 * rank)
-
-    def exchange(ks):
-        return [
-            push(st.at[kind(flip(r, k))], xg.at[r], xs.at[k], xr.at[k], mate(k)) for k in ks
-        ]
-
-    shares = exchange((1, 2, 3))
-    xg[r] = st[kind(r)]
+    shares = []
+    for k in range(1, PLANE):
+        src = st.at[flip(r, k) % PLANE]
+        shares.append(push(src, xg.at[r], xs.at[k], xr.at[k], mate(k)))
+    xg[r] = st[r % PLANE]
+
+    def lift(k):
+        at = flip(r, k)
+        return push(xg.at[at], xg.at[at], zs.at[k], zr.at[k], mate(PLANE))
 
     causal = lax.broadcasted_iota(jnp.int32, (span, span), 0) <= lax.broadcasted_iota(
         jnp.int32, (span, span), 1
@@ -199,6 +198,36 @@
     def part(c, start, count):
         rows = slice(start, start + count)
         return jnp.concatenate([rec[2 * c, rows, :], rec[2 * c + 1, rows, :]], 1)
+
+    def relay(src, dst, send, recv, sign):
+        for d in range(1, ng):
+            to = g + sign * d
+
+            @pl.when((to >= 0) & (to < ng))
+            def _():
+                push(src, dst.at[d], send.at[d], recv.at[d], (to * H + r, core))
+
+    def settle(src, dst, send, recv, sign):
+        for d in range(1, ng):
+            to = g + sign * d
+
+            @pl.when((to >= 0) & (to < ng))
+            def _():
+                pltpu.make_async_remote_copy(
+                    src, dst.at[d], send.at[d], recv.at[d], (to * H + r, core), MESH
+                ).wait_send()
+
+    def collect(src, dst, send, recv, sign, total):
+        total[...] = jnp.zeros(total.shape, F32)
+        for d in range(1, ng):
+            frm = g - sign * d
+
+            @pl.when((frm >= 0) & (frm < ng))
+            def _():
+                pltpu.make_async_remote_copy(
+                    src, dst.at[d], send.at[d], recv.at[d], (frm * H + r, core), MESH
+                ).wait_recv()
+                total[...] += dst[d]
 
     for copy in ups + qkv:
         copy.wait_recv()
@@ -218,11 +247,8 @@
         values = values + dot(fk, va[:DV], (1, 1))
         norms = norms + dot(va[DV:], fk, (1, 1))
     ssend[...] = pack(values, norms)
-    states = []
-    for d in range(1, ng):
-        to = (((g + d) % ng) * H + r, core)
-        states.append(push(ssend, srecv.at[d], ss.at[d], sr.at[d], to))
-    shares += exchange((4, 5))
+    relay(ssend, srecv, ss, sr, 1)
+    lifts = [lift(0)]
 
     for c in range(chunks):
         fq, fk, va = fqs[c], fks[c], vas[c]
@@ -236,13 +262,9 @@
             )
         tops[c] = top
 
-    packed = jnp.zeros(ssend.shape, F32)
-    for d, copy in enumerate(states, 1):
-        copy.wait_recv()
-        packed = packed + jnp.where((g - d + ng) % ng < g, srecv[d], 0.0)
-    in_values, in_norms = unpack(packed)
+    collect(ssend, srecv, ss, sr, 1, sin)
+    in_values, in_norms = unpack(sin[...])
     in_pair, in_norm_pair = halves(in_values), halves(in_norms)
-
     back = jnp.zeros((FEATS, DV), F32)
     back_norm = jnp.zeros((AUX, FEATS), F32)
     back_norm_at = [None] * chunks
@@ -262,11 +284,9 @@
         back = back + dot2r(fq, (gn[0][:DV], gn[1][:DV]), (1, 1))
         back_norm = back_norm + dot2((gn[0][DV:], gn[1][DV:]), fq, (1, 1))
     rsend[...] = pack(back, back_norm)
-    backs = []
-    for d in range(1, ng):
-        to = (((g + d) % ng) * H + r, core)
-        backs.append(push(rsend, rrecv.at[d], rs.at[d], rr.at[d], to))
-    shares += exchange((6, 7))
+    relay(rsend, rrecv, rs, rr, -1)
+    shares[0].wait_recv()
+    lifts.append(lift(1))
 
     def store(c, start, rows):
         half = 0 if start < HALF else 1
@@ -295,16 +315,16 @@
         gvs[c] = gv
         gfks[c] = gfk
 
-    base = (r // 4) * 4
-    for copy in shares[:3]:
-        copy.wait_recv()
-    pairs = [push(xg.at[pl.ds(base, 4)], xp.at[pl.ds(base, 4)], ps.at[0], pr.at[0], (seq, other))]
-
-    packed = jnp.zeros(rsend.shape, F32)
-    for d, copy in enumerate(backs, 1):
-        copy.wait_recv()
-        packed = packed + jnp.where((g - d + ng) % ng > g, rrecv[d], 0.0)
-    in_values, in_norms = unpack(packed)
+    for k in range(2, PLANE):
+        shares[k - 1].wait_recv()
+        lifts.append(lift(k))
+    base = (r // PLANE) * PLANE
+    near = push(
+        xg.at[pl.ds(base, PLANE)], xp.at[pl.ds(base, PLANE)], ps.at[0], pr.at[0], (seq, other)
+    )
+
+    collect(rsend, rrecv, rs, rr, -1, rin)
+    in_values, in_norms = unpack(rin[...])
     in_pair, in_norm_pair = halves(in_values), halves(in_norms)
     for c in range(chunks):
         fk, va = fks[c], vas[c]
@@ -314,62 +334,96 @@
         store(c, HALF + DK, gv[DV // 2 :])
         store(c, HALF, pull(part(c, DK, DK) * 0.5, gfk) * 0.5)
 
-    gathers = []
-    for i in range(PIECES):
-        row = []
-        for n, bit in enumerate(BITS, 1):
+    pending = [near] + shares + ups + qkv
+
+    def direct(i):
+        rows = pl.ds(i * ROWS, ROWS)
+        for k in (1, 2):
             for half in range(2):
-                row.append(
+                pending.append(
                     push(
-                        o.at[:, half, pl.ds(i * ROWS, ROWS)],
-                        gj.at[i, n, core],
-                        gs.at[i, n, half],
-                        gr.at[i, n, core],
-                        (g * H + flip(r, bit), half),
+                        o.at[:, half, rows], gj.at[i, k, core], gs.at[i, k, half],
+                        gr.at[i, k, core], (g * H + flip(r, k), half),
                     )
                 )
-        row.append(
+        pending.append(
             push(
-                o.at[:, other, pl.ds(i * ROWS, ROWS)],
-                gj.at[i, 0, core],
-                gs.at[i, 0, 0],
-                gr.at[i, 0, core],
+                o.at[:, other, rows], gj.at[i, 0, core], gs.at[i, 0, 0],
+                gr.at[i, 0, core], (seq, other),
+            )
+        )
+
+    def arrive(i, k, b):
+        pltpu.make_async_copy(gj.at[i, k, b], gj.at[i, k, b], gr.at[i, k, b]).wait()
+
+    def forward(i):
+        k = 1 + i % 2
+        for b in range(2):
+            arrive(i, k, b)
+        for b in range(2):
+            pending.append(
+                push(
+                    gj.at[i, k, b], gj.at[i, PLANE - 1, b], hs.at[i, b],
+                    gr.at[i, PLANE - 1, b], mate(PLANE - 1 - k),
+                )
+            )
+
+    direct(0)
+    direct(1)
+    for i in range(PIECES):
+        gj[i, 0, core] = o[:, core, i * ROWS : (i + 1) * ROWS, :]
+    near.wait_recv()
+    for j in range(PLANE):
+        at = base + j
+        rows = pl.ds(pl.multiple_of(at * length, length), length)
+        xb[core, rows, :] = xg[at].astype(BF)
+        xb[other, rows, :] = xp[at].astype(BF)
+    forward(0)
+    direct(2)
+    for k in range(PLANE):
+        lifts[k].wait_recv()
+        at = flip(mirror, k)
+        pending.append(push(xg.at[at], xp.at[at], ps.at[1 + k], pr.at[1 + k], (seq, other)))
+    for k in range(PLANE):
+        at = flip(mirror, k)
+        rows = pl.ds(pl.multiple_of(at * length, length), length)
+        xb[core, rows, :] = xg[at].astype(BF)
+    for k in range(PLANE):
+        pending[k - PLANE].wait_recv()
+        at = flip(mirror, k)
+        rows = pl.ds(pl.multiple_of(at * length, length), length)
+        xb[other, rows, :] = xp[at].astype(BF)
+    pending += lifts
+
+    tokens = 2 * H * length
+    sent = []
+    for i in range(PIECES):
+        if i + 1 < PIECES:
+            forward(i + 1)
+            if i + 3 < PIECES:
+                direct(i + 3)
+        for b in range(2):
+            arrive(i, 2 - i % 2, b)
+            arrive(i, PLANE - 1, b)
+        arrive(i, 0, other)
+        pending.append(
+            push(
+                gj.at[i, :, other, r], rt.at[0, core, i], ts.at[0, i, 0], tr.at[0, i, 0],
                 (seq, other),
             )
         )
-        gathers.append(row)
-    returns = []
-    for k in range(1, H):
-        returns.append(push(o.at[flip(r, k)], ret.at[r], ts.at[k], tr.at[k], mate(k)))
-    ret[r] = o[r]
-    for i in range(PIECES):
-        gj[i, 0, core] = o[:, core, i * ROWS : (i + 1) * ROWS, :]
-
-    for copy in shares[3:]:
-        copy.wait_recv()
-    far = 4 - base
-    pairs.append(push(xg.at[pl.ds(far, 4)], xp.at[pl.ds(far, 4)], ps.at[1], pr.at[1], (seq, other)))
-    for j in range(H):
-        xb[core, j * length : (j + 1) * length, :] = xg[j].astype(BF)
-    for copy in pairs:
-        copy.wait_recv()
-    for j in range(H):
-        xb[other, j * length : (j + 1) * length, :] = xp[j].astype(BF)
-
-    def arrive(i, n, b):
-        return pltpu.make_async_copy(gj.at[i, n, b], gj.at[i, n, b], gr.at[i, n, b])
-
-    tokens = 2 * H * length
-    sent = []
-    for i in range(PIECES):
-        for n in range(1, 1 + len(BITS)):
-            for b in range(2):
-                arrive(i, n, b).wait()
-        arrive(i, 0, other).wait()
+        for b in range(2):
+            pending.append(
+                push(
+                    gj.at[i, :, b, mirror], rt.at[1, core, i], ts.at[1, i, b],
+                    tr.at[1, i, core], (g * H + mirror, b),
+                )
+            )
+        rt[0, core, i] = gj[i, :, core, r]
         rows = []
-        for n in range(1 + len(BITS)):
+        for k in range(PLANE):
             rows.append(
-                jnp.concatenate([gj[i, n, b, j] for b in range(2) for j in range(H)], 1)
+                jnp.concatenate([gj[i, k, b, j] for b in range(2) for j in range(H)], 1)
             )
         grads = jnp.concatenate(rows, 0).astype(BF)
         product = dot(grads, xb[...].reshape(tokens, slots * owned), (1, 0))
@@ -381,8 +435,8 @@
                 if d == 0 and w == 0:
                     continue
                 group = (g + d) % ng
-                rank = r if w == 0 else anti
-                slot = group * 2 + rank // 4
+                rank = r if w == 0 else mirror
+                slot = group * 2 + rank // PLANE
                 row.append(
                     push(
                         ls.at[i, slot], lr.at[i, d, w], bs.at[i, d, w], br.at[i, d, w],
@@ -391,13 +445,20 @@
                 )
         sent.append(row)
 
-    for copy in returns:
-        copy.wait_recv()
-    blocks = []
-    for n in range(2):
-        blocks.append(jnp.concatenate([ret[h, n, :DK, :] for h in range(H)], 0))
+    for i in range(PIECES):
+        pltpu.make_async_copy(rt.at[0, other, i], rt.at[0, other, i], tr.at[0, i, 0]).wait()
+        for b in range(2):
+            pltpu.make_async_copy(rt.at[1, b, i], rt.at[1, b, i], tr.at[1, i, b]).wait()
+
+    def back_rows(h, half):
+        low = [((h // bit + r // bit) % 2) * bit for bit in (1, 2)]
+        place = (h // PLANE + r // PLANE) % 2
+        return jnp.concatenate([rt[place, half, i, low[0] + low[1]] for i in range(PIECES)], 0)
+
+    whole = [[back_rows(h, half) for half in range(2)] for h in range(H)]
+    blocks = [jnp.concatenate([whole[h][n][:DK] for h in range(H)], 0) for n in range(2)]
     for h in range(H):
-        blocks.append(jnp.concatenate([ret[h, 0, DK:, :], ret[h, 1, DK:, :]], 0))
+        blocks.append(jnp.concatenate([whole[h][0][DK:], whole[h][1][DK:]], 0))
     for n, block in enumerate(blocks):
         jt[:, n * DV : (n + 1) * DV] = block.T.astype(BF)
     step = 512
@@ -412,37 +473,37 @@
     for i in range(PIECES):
         for copy in sent[i]:
             copy.wait_recv()
-        mine = ls[i, g * 2 + r // 4]
+        mine = ls[i, g * 2 + r // PLANE]
         rest = lr[i, 0, 1]
         for d in range(1, ng):
             mine = mine + lr[i, d, 0]
             rest = rest + lr[i, d, 1]
-        for n, bit in enumerate((0,) + BITS):
-            f2[core, i, flip(r, bit)] = mine[n * ROWS : (n + 1) * ROWS]
-            f2[core, i, flip(anti, bit)] = rest[n * ROWS : (n + 1) * ROWS]
-        swaps.append(
-            push(f2.at[core, i], f2.at[core, i], ds.at[i], dr.at[i], (seq, other))
-        )
+        for k in range(PLANE):
+            f2[core, i, flip(r, k)] = mine[k * ROWS : (k + 1) * ROWS]
+            f2[core, i, flip(mirror, k)] = rest[k * ROWS : (k + 1) * ROWS]
+        swaps.append(push(f2.at[core, i], f2.at[core, i], ds.at[i], dr.at[i], (seq, other)))
     for copy in swaps:
         copy.wait_recv()
-    final = []
-    for n in range(2):
-        final.append(jnp.concatenate([f2[n, 0, h, :DK] for h in range(H)], 0))
+    final = [jnp.concatenate([f2[n, 0, h, :DK] for h in range(H)], 0) for n in range(2)]
     for h in range(H):
         parts = []
         for n in range(2):
             for i in range(PIECES):
-                parts.append(f2[n, i, h, DK if i == 0 else 0 :])
+                start = max(DK - i * ROWS, 0)
+                if start < ROWS:
+                    parts.append(f2[n, i, h, start:])
         final.append(jnp.concatenate(parts, 0))
     keep = owned // 2
     for n, block in enumerate(final):
         fs[n] = block.T
         out_ref[n] = fs[n, pl.ds(pl.multiple_of(core * keep, keep), keep), :]
-    everything += ups + qkv + shares + states + backs + pairs + returns + swaps
-    for row in gathers + sent:
-        everything += row
-    for copy in everything:
+    pending += swaps
+    for row in sent:
+        pending += row
+    for copy in pending:
         copy.wait_send()
+    settle(ssend, srecv, ss, sr, 1)
+    settle(rsend, rrecv, rs, rr, -1)
 
 
 def fused(tokens, upstream, weights, ng):
@@ -452,27 +513,28 @@
     chunks, span = H // 2, 2 * length
     vm = lambda *shape: pltpu.VMEM(shape, F32)
     half = lambda *shape: pltpu.VMEM(shape, BF)
-    nb = 1 + len(BITS)
+    state = (FEATS + 16, DV)
     scratch = [half(length, width), half(length, H * DV)]
     scratch += [pltpu.VMEM(w.shape, w.dtype) for w in weights]
     scratch += [
         vm(H, 2 * DK + 2 * DV, length), vm(H, 2 * DK + 2 * DV, length),
-        vm(H // 2, length, slots * owned), vm(H, length, slots * owned),
+        vm(PLANE, length, slots * owned), vm(H, length, slots * owned),
         vm(H, length, slots * owned), half(2, H * length, slots * owned),
         half(chunks, FEATS, span), half(chunks, FEATS, span), half(chunks, DV + AUX, span),
         half(chunks, span, span), half(chunks, span, span),
         half(chunks, DV + AUX, span), half(chunks, DV + AUX, span),
         vm(chunks, DV + AUX, span), vm(chunks, FEATS, DV), vm(chunks, FEATS, DV),
         vm(chunks, DV, span), vm(chunks, FEATS, span),
-        vm(FEATS + 16, DV), vm(ng, FEATS + 16, DV), vm(FEATS + 16, DV), vm(ng, FEATS + 16, DV),
-        vm(H, 2, HALF, length), vm(PIECES, nb, 2, H, ROWS, length),
-        vm(PIECES, slots, nb * ROWS, owned), vm(PIECES, ng, 2, nb * ROWS, owned),
-        vm(H, 2, HALF, length), half(length, H * DV + 2 * DV),
+        vm(*state), vm(ng, *state), vm(*state), vm(*state), vm(ng, *state), vm(*state),
+        vm(H, 2, HALF, length), vm(PIECES, PLANE, 2, H, ROWS, length),
+        vm(PIECES, slots, PLANE * ROWS, owned), vm(PIECES, ng, 2, PLANE * ROWS, owned),
+        vm(2, 2, PIECES, PLANE, ROWS, length), half(length, H * DV + 2 * DV),
         vm(2, PIECES, H, ROWS, owned), vm(2 + H, owned, DV),
         sems(5),
-        sems(H), sems(H), sems(H), sems(H), sems(H), sems(H), sems(2), sems(2),
-        sems(ng), sems(ng), sems(ng), sems(ng),
-        sems(PIECES, nb, 2), sems(PIECES, nb, 2), sems(H), sems(H),
+        sems(H), sems(H), sems(H), sems(H), sems(PLANE), sems(PLANE), sems(PLANE), sems(PLANE),
+        sems(1 + PLANE), sems(1 + PLANE), sems(ng), sems(ng), sems(ng), sems(ng),
+        sems(PIECES, PLANE, 2), sems(PIECES, PLANE, 2), sems(PIECES, 2),
+        sems(2, PIECES, 2), sems(2, PIECES, 2),
         sems(PIECES, ng, 2), sems(PIECES, ng, 2), sems(PIECES), sems(PIECES),
     ]
     return pl.pallas_call(

time: 89 us -> 78.3 us (0.88)
  Pallas kernels: 88 us -> 77.5 us
    pallas_call x1, Pallas kernels: 86 us -> 75.5 us  [fused(): pl.pallas_call(functools.partial(fused_kernel, ng), out_shape=[jax.ShapeD...]
where the time goes in v2:
time: 78.3 us; the launch traced here: 78.2 us
  Pallas kernels  77.5 us (99%)
    pallas_call x1, Pallas kernels, fused(): pl.pallas_call(functools.partial(fused_kernel, ng), out_shape=[jax.ShapeD...  75.5 us
    pallas_call x1, Pallas kernels, finish(): pl.pallas_call(finish_kernel, out_shape=[jax.ShapeDtypeStruct((1,) + grad...  2.06 us

profile of v2, /device:TPU:0, one launch (start us, length us, event | category | flops | bytes accessed | tf_op | source)
XLA Modules:
  0.0 78.2 jit_solution(9437578698327023330)
XLA Ops:
  0.6 75.5 %shard_map.84 = (bf16[128,2048]{1,0:T(8,128)(2,1)}, f32[10,64,128]{2,1,0:T(8,128)}) custom-call(bf16[128,2048]{1,0:T(8,128)(2,1)} %bitcast.2, bf16[128,1024]{1,0:T(8,128)(2,1)} %bitcast.3, bf16[2048,128]{1,0:T(8,128)(2,1)} %wq_hbm.1, bf16[2048,128]{1,0:T(8,128)(2,1)} %wk_hbm.1, bf16[2048,1024]{1,0:T(8,128)(2,1)} %wv_hbm.1), custom_call_target="tpu_custom_call" | custom-call | tf_op jit(solution)/shard_map/pallas_call | solution.py:540
  76.1 2.1 %shard_map.85 = (bf16[1,128,2048]{2,1,0:T(8,128)(2,1)}, f32[64,128]{1,0:T(8,128)}, f32[64,128]{1,0:T(8,128)}, f32[64,1024]{1,0:T(8,128)}) custom-call(bf16[128,2048]{1,0:T(8,128)(2,1)} %get-tuple-element.6.gi_ref, f32[10,64,128]{2,1,0:T(8,128)} %get-tuple-element.7.o_ref), custom_call_target="tpu_custom_call" | custom-call | tf_op jit(solution)/shard_map/pallas_call | solution.py:565

commit v3 on v2

--- a/solution.py
+++ b/solution.py
@@ -113,9 +113,9 @@
     ng, x_hbm, c_hbm, wq_hbm, wk_hbm, wv_hbm, gi_ref, out_ref,
     x_ref, c_ref, wq_ref, wk_ref, wv_ref, own, rec, st, xg, xp, xb,
     fqs, fks, vas, ah, al, nh, nl, tops, pv, rv, gvs, gfks,
-    ssend, srecv, sin, rsend, rrecv, rin, o, gj, ls, lr, rt, jt, f2, fs,
-    load, us, ur, qs, qr, xs, xr, zs, zr, ps, pr, ss, sr, rs, rr,
-    gs, gr, hs, ts, tr, bs, br, ds, dr,
+    ssend, srecv, sin, rsend, rrecv, rin, o, gj, ls, lr, acc, l2, rt, jt, f2, fs,
+    load, us, ur, qs, qr, xs, xr, ps, pr, ss, sr, rs, rr,
+    zs, gs, gr, hs, ts, tr, bs, br, cs, cr, ds, dr,
 ):
     seq = lax.axis_index("seq")
     core = lax.axis_index("batch")
@@ -145,7 +145,7 @@
     peers += [(g * H + flip(r, bit), other) for bit in BITS]
     for d in range(1, ng):
         far = (g + d) % ng
-        peers += [(far * H + r, core), (far * H + mirror, core)]
+        peers.append((far * H + r, core))
     barrier = pltpu.get_barrier_semaphore()
     for peer in peers:
         pl.semaphore_signal(barrier, inc=1, device_id=peer, device_id_type=MESH)
@@ -185,10 +185,6 @@
         shares.append(push(src, xg.at[r], xs.at[k], xr.at[k], mate(k)))
     xg[r] = st[r % PLANE]
 
-    def lift(k):
-        at = flip(r, k)
-        return push(xg.at[at], xg.at[at], zs.at[k], zr.at[k], mate(PLANE))
-
     causal = lax.broadcasted_iota(jnp.int32, (span, span), 0) <= lax.broadcasted_iota(
         jnp.int32, (span, span), 1
     )
@@ -248,7 +244,6 @@
         norms = norms + dot(va[DV:], fk, (1, 1))
     ssend[...] = pack(values, norms)
     relay(ssend, srecv, ss, sr, 1)
-    lifts = [lift(0)]
 
     for c in range(chunks):
         fq, fk, va = fqs[c], fks[c], vas[c]
@@ -285,9 +280,6 @@
         back_norm = back_norm + dot2((gn[0][DV:], gn[1][DV:]), fq, (1, 1))
     rsend[...] = pack(back, back_norm)
     relay(rsend, rrecv, rs, rr, -1)
-    shares[0].wait_recv()
-    lifts.append(lift(1))
-
     def store(c, start, rows):
         half = 0 if start < HALF else 1
         at = start - half * HALF
@@ -315,9 +307,8 @@
         gvs[c] = gv
         gfks[c] = gfk
 
-    for k in range(2, PLANE):
-        shares[k - 1].wait_recv()
-        lifts.append(lift(k))
+    for copy in shares:
+        copy.wait_recv()
     base = (r // PLANE) * PLANE
     near = push(
         xg.at[pl.ds(base, PLANE)], xp.at[pl.ds(base, PLANE)], ps.at[0], pr.at[0], (seq, other)
@@ -335,6 +326,20 @@
         store(c, HALF, pull(part(c, DK, DK) * 0.5, gfk) * 0.5)
 
     pending = [near] + shares + ups + qkv
+    here = pl.ds(base, PLANE)
+    there = pl.ds(PLANE - base, PLANE)
+    place = r % PLANE
+    side = r // PLANE
+
+    def across(i):
+        rows = pl.ds(i * ROWS, ROWS)
+        for half in range(2):
+            pending.append(
+                push(
+                    o.at[there, half, rows], gj.at[i, 1, 0, core], zs.at[i, half],
+                    gr.at[i, 1, 0, core], (g * H + mirror, half),
+                )
+            )
 
     def direct(i):
         rows = pl.ds(i * ROWS, ROWS)
@@ -342,118 +347,136 @@
             for half in range(2):
                 pending.append(
                     push(
-                        o.at[:, half, rows], gj.at[i, k, core], gs.at[i, k, half],
-                        gr.at[i, k, core], (g * H + flip(r, k), half),
+                        o.at[here, half, rows], gj.at[i, 0, k, core], gs.at[i, 0, k, half],
+                        gr.at[i, 0, k, core], (g * H + flip(r, k), half),
                     )
                 )
         pending.append(
             push(
-                o.at[:, other, rows], gj.at[i, 0, core], gs.at[i, 0, 0],
-                gr.at[i, 0, core], (seq, other),
+                o.at[here, other, rows], gj.at[i, 0, 0, core], gs.at[i, 0, 0, 0],
+                gr.at[i, 0, 0, core], (seq, other),
             )
         )
 
-    def arrive(i, k, b):
-        pltpu.make_async_copy(gj.at[i, k, b], gj.at[i, k, b], gr.at[i, k, b]).wait()
-
-    def forward(i):
-        k = 1 + i % 2
-        for b in range(2):
-            arrive(i, k, b)
-        for b in range(2):
+    def landed(ref, sem):
+        pltpu.make_async_copy(ref, ref, sem).wait()
+
+    def arrive(i, m, k):
+        if m == 0 or k == 0:
+            if k < PLANE - 1:
+                for b in range(2):
+                    landed(gj.at[i, m, k, b], gr.at[i, m, k, b])
+                return
+        landed(gj.at[i, m, k], gr.at[i, m, k, 0])
+
+    def mirrored(i):
+        arrive(i, 1, 0)
+        for k in (1, 2):
             pending.append(
                 push(
-                    gj.at[i, k, b], gj.at[i, PLANE - 1, b], hs.at[i, b],
-                    gr.at[i, PLANE - 1, b], mate(PLANE - 1 - k),
+                    gj.at[i, 1, 0], gj.at[i, 1, k], gs.at[i, 1, k, 0], gr.at[i, 1, k, 0], mate(k)
                 )
             )
 
-    direct(0)
-    direct(1)
-    for i in range(PIECES):
-        gj[i, 0, core] = o[:, core, i * ROWS : (i + 1) * ROWS, :]
-    near.wait_recv()
-    for j in range(PLANE):
-        at = base + j
-        rows = pl.ds(pl.multiple_of(at * length, length), length)
-        xb[core, rows, :] = xg[at].astype(BF)
-        xb[other, rows, :] = xp[at].astype(BF)
-    forward(0)
-    direct(2)
-    for k in range(PLANE):
-        lifts[k].wait_recv()
-        at = flip(mirror, k)
-        pending.append(push(xg.at[at], xp.at[at], ps.at[1 + k], pr.at[1 + k], (seq, other)))
-    for k in range(PLANE):
-        at = flip(mirror, k)
-        rows = pl.ds(pl.multiple_of(at * length, length), length)
-        xb[core, rows, :] = xg[at].astype(BF)
-    for k in range(PLANE):
-        pending[k - PLANE].wait_recv()
-        at = flip(mirror, k)
-        rows = pl.ds(pl.multiple_of(at * length, length), length)
-        xb[other, rows, :] = xp[at].astype(BF)
-    pending += lifts
-
-    tokens = 2 * H * length
-    sent = []
-    for i in range(PIECES):
-        if i + 1 < PIECES:
-            forward(i + 1)
-            if i + 3 < PIECES:
-                direct(i + 3)
-        for b in range(2):
-            arrive(i, 2 - i % 2, b)
-            arrive(i, PLANE - 1, b)
-        arrive(i, 0, other)
+    def turn(i, m):
+        return 1 + (i + m) % 2
+
+    def forward(i, m):
+        k = turn(i, m)
+        arrive(i, m, k)
         pending.append(
             push(
-                gj.at[i, :, other, r], rt.at[0, core, i], ts.at[0, i, 0], tr.at[0, i, 0],
+                gj.at[i, m, k], gj.at[i, m, PLANE - 1], hs.at[i, m],
+                gr.at[i, m, PLANE - 1, 0], mate(PLANE - 1 - k),
+            )
+        )
+
+    def multiply(i, m):
+        arrive(i, m, PLANE - 1 - turn(i, m))
+        arrive(i, m, PLANE - 1)
+        if m == 0:
+            landed(gj.at[i, 0, 0, other], gr.at[i, 0, 0, other])
+        pending.append(
+            push(
+                gj.at[i, m, :, other, place], rt.at[core, i, m], ts.at[i, m], tr.at[i, m],
                 (seq, other),
             )
         )
-        for b in range(2):
-            pending.append(
-                push(
-                    gj.at[i, :, b, mirror], rt.at[1, core, i], ts.at[1, i, b],
-                    tr.at[1, i, core], (g * H + mirror, b),
-                )
-            )
-        rt[0, core, i] = gj[i, :, core, r]
+        rt[core, i, m] = gj[i, m, :, core, place]
         rows = []
         for k in range(PLANE):
             rows.append(
-                jnp.concatenate([gj[i, k, b, j] for b in range(2) for j in range(H)], 1)
+                jnp.concatenate([gj[i, m, k, b, j] for b in range(2) for j in range(PLANE)], 1)
             )
         grads = jnp.concatenate(rows, 0).astype(BF)
-        product = dot(grads, xb[...].reshape(tokens, slots * owned), (1, 0))
+        product = dot(grads, xb[...].reshape(2 * PLANE * length, slots * owned), (1, 0))
         for a in range(slots):
-            ls[i, a] = product[:, a * owned : (a + 1) * owned]
-        row = []
-        for d in range(ng):
-            for w in range(2):
-                if d == 0 and w == 0:
-                    continue
-                group = (g + d) % ng
-                rank = r if w == 0 else mirror
-                slot = group * 2 + rank // PLANE
-                row.append(
-                    push(
-                        ls.at[i, slot], lr.at[i, d, w], bs.at[i, d, w], br.at[i, d, w],
-                        (group * H + rank, core),
-                    )
-                )
-        sent.append(row)
-
+            ls[i, m, a % 2, a // 2] = product[:, a * owned : (a + 1) * owned]
+        pending.append(
+            push(
+                ls.at[i, m, 1 - side], lr.at[i, 1 - m], bs.at[i, m], br.at[i, 1 - m], mate(PLANE)
+            )
+        )
+
+    def combine(i):
+        for m in range(2):
+            landed(lr.at[i, m], br.at[i, m])
+            for a in range(ng):
+                acc[i, a, m] = ls[i, m, side, a] + lr[i, m, a]
+        for d in range(1, ng):
+            to = (g + d) % ng
+            pending.append(
+                push(acc.at[i, to], l2.at[i, d], cs.at[i, d], cr.at[i, d], (to * H + r, core))
+            )
+
+    swaps = []
+
+    def settled(i):
+        total = acc[i, g]
+        for d in range(1, ng):
+            landed(l2.at[i, d], cr.at[i, d])
+            total = total + l2[i, d]
+        for m in range(2):
+            for k in range(PLANE):
+                rows = total[m, k * ROWS : (k + 1) * ROWS]
+                f2[core, i, flip(mirror if m else r, k)] = rows
+        swaps.append(push(f2.at[core, i], f2.at[core, i], ds.at[i], dr.at[i], (seq, other)))
+
+    across(0)
+    direct(0)
+    across(1)
+    direct(1)
+    for i in range(2, PIECES):
+        across(i)
     for i in range(PIECES):
-        pltpu.make_async_copy(rt.at[0, other, i], rt.at[0, other, i], tr.at[0, i, 0]).wait()
-        for b in range(2):
-            pltpu.make_async_copy(rt.at[1, b, i], rt.at[1, b, i], tr.at[1, i, b]).wait()
+        gj[i, 0, 0, core] = o[here, core, i * ROWS : (i + 1) * ROWS, :]
+    near.wait_recv()
+    for j in range(PLANE):
+        xb[core, j * length : (j + 1) * length, :] = xg[base + j].astype(BF)
+        xb[other, j * length : (j + 1) * length, :] = xp[base + j].astype(BF)
+    mirrored(0)
+    forward(0, 0)
+    for i in range(PIECES):
+        if i + 1 < PIECES:
+            mirrored(i + 1)
+            forward(i + 1, 0)
+        if i + 2 < PIECES:
+            direct(i + 2)
+        forward(i, 1)
+        multiply(i, 0)
+        multiply(i, 1)
+        if i > 0:
+            combine(i - 1)
+        if i > 1:
+            settled(i - 2)
+    for i in range(PIECES):
+        for m in range(2):
+            landed(rt.at[other, i, m], tr.at[i, m])
 
     def back_rows(h, half):
         low = [((h // bit + r // bit) % 2) * bit for bit in (1, 2)]
-        place = (h // PLANE + r // PLANE) % 2
-        return jnp.concatenate([rt[place, half, i, low[0] + low[1]] for i in range(PIECES)], 0)
+        m = (h // PLANE + r // PLANE) % 2
+        return jnp.concatenate([rt[half, i, m, low[0] + low[1]] for i in range(PIECES)], 0)
 
     whole = [[back_rows(h, half) for half in range(2)] for h in range(H)]
     blocks = [jnp.concatenate([whole[h][n][:DK] for h in range(H)], 0) for n in range(2)]
@@ -469,19 +492,9 @@
         total = total + dot(jt[:, 2 * DV :], wv_ref[rows, :], (1, 1))
         gi_ref[:, rows] = total.astype(BF)
 
-    swaps = []
-    for i in range(PIECES):
-        for copy in sent[i]:
-            copy.wait_recv()
-        mine = ls[i, g * 2 + r // PLANE]
-        rest = lr[i, 0, 1]
-        for d in range(1, ng):
-            mine = mine + lr[i, d, 0]
-            rest = rest + lr[i, d, 1]
-        for k in range(PLANE):
-            f2[core, i, flip(r, k)] = mine[k * ROWS : (k + 1) * ROWS]
-            f2[core, i, flip(mirror, k)] = rest[k * ROWS : (k + 1) * ROWS]
-        swaps.append(push(f2.at[core, i], f2.at[core, i], ds.at[i], dr.at[i], (seq, other)))
+    combine(PIECES - 1)
+    for i in range(PIECES - 2, PIECES):
+        settled(i)
     for copy in swaps:
         copy.wait_recv()
     final = [jnp.concatenate([f2[n, 0, h, :DK] for h in range(H)], 0) for n in range(2)]
@@ -498,8 +511,6 @@
         fs[n] = block.T
         out_ref[n] = fs[n, pl.ds(pl.multiple_of(core * keep, keep), keep), :]
     pending += swaps
-    for row in sent:
-        pending += row
     for copy in pending:
         copy.wait_send()
     settle(ssend, srecv, ss, sr, 1)
@@ -519,23 +530,24 @@
     scratch += [
         vm(H, 2 * DK + 2 * DV, length), vm(H, 2 * DK + 2 * DV, length),
         vm(PLANE, length, slots * owned), vm(H, length, slots * owned),
-        vm(H, length, slots * owned), half(2, H * length, slots * owned),
+        vm(H, length, slots * owned), half(2, PLANE * length, slots * owned),
         half(chunks, FEATS, span), half(chunks, FEATS, span), half(chunks, DV + AUX, span),
         half(chunks, span, span), half(chunks, span, span),
         half(chunks, DV + AUX, span), half(chunks, DV + AUX, span),
         vm(chunks, DV + AUX, span), vm(chunks, FEATS, DV), vm(chunks, FEATS, DV),
         vm(chunks, DV, span), vm(chunks, FEATS, span),
         vm(*state), vm(ng, *state), vm(*state), vm(*state), vm(ng, *state), vm(*state),
-        vm(H, 2, HALF, length), vm(PIECES, PLANE, 2, H, ROWS, length),
-        vm(PIECES, slots, PLANE * ROWS, owned), vm(PIECES, ng, 2, PLANE * ROWS, owned),
-        vm(2, 2, PIECES, PLANE, ROWS, length), half(length, H * DV + 2 * DV),
+        vm(H, 2, HALF, length), vm(PIECES, 2, PLANE, 2, PLANE, ROWS, length),
+        vm(PIECES, 2, 2, ng, PLANE * ROWS, owned), vm(PIECES, 2, ng, PLANE * ROWS, owned),
+        vm(PIECES, ng, 2, PLANE * ROWS, owned), vm(PIECES, ng, 2, PLANE * ROWS, owned),
+        vm(2, PIECES, 2, PLANE, ROWS, length), half(length, H * DV + 2 * DV),
         vm(2, PIECES, H, ROWS, owned), vm(2 + H, owned, DV),
         sems(5),
-        sems(H), sems(H), sems(H), sems(H), sems(PLANE), sems(PLANE), sems(PLANE), sems(PLANE),
-        sems(1 + PLANE), sems(1 + PLANE), sems(ng), sems(ng), sems(ng), sems(ng),
-        sems(PIECES, PLANE, 2), sems(PIECES, PLANE, 2), sems(PIECES, 2),
-        sems(2, PIECES, 2), sems(2, PIECES, 2),
-        sems(PIECES, ng, 2), sems(PIECES, ng, 2), sems(PIECES), sems(PIECES),
+        sems(H), sems(H), sems(H), sems(H), sems(PLANE), sems(PLANE),
+        sems(1), sems(1), sems(ng), sems(ng), sems(ng), sems(ng),
+        sems(PIECES, 2), sems(PIECES, 2, PLANE, 2), sems(PIECES, 2, PLANE, 2), sems(PIECES, 2),
+        sems(PIECES, 2), sems(PIECES, 2), sems(PIECES, 2), sems(PIECES, 2),
+        sems(PIECES, ng), sems(PIECES, ng), sems(PIECES), sems(PIECES),
     ]
     return pl.pallas_call(
         functools.partial(fused_kernel, ng),

time: 78.3 us -> 84.9 us (1.084)
  Pallas kernels: 77.5 us -> 83.8 us
    pallas_call x1, Pallas kernels: 75.5 us -> 81.8 us  [fused(): pl.pallas_call(functools.partial(fused_kernel, ng), out_shape=[jax.ShapeD...]
where the time goes in v3:
time: 84.9 us; the launch traced here: 84.4 us
  Pallas kernels  83.8 us (99%)
    pallas_call x1, Pallas kernels, fused(): pl.pallas_call(functools.partial(fused_kernel, ng), out_shape=[jax.ShapeD...  81.8 us
    pallas_call x1, Pallas kernels, finish(): pl.pallas_call(finish_kernel, out_shape=[jax.ShapeDtypeStruct((1,) + grad...  2.06 us

profile of v3, /device:TPU:0, one launch (start us, length us, event | category | flops | bytes accessed | tf_op | source)
XLA Modules:
  0.0 84.4 jit_solution(8963755984526328565)
XLA Ops:
  0.6 81.8 %shard_map.84 = (bf16[128,2048]{1,0:T(8,128)(2,1)}, f32[10,64,128]{2,1,0:T(8,128)}) custom-call(bf16[128,2048]{1,0:T(8,128)(2,1)} %bitcast.2, bf16[128,1024]{1,0:T(8,128)(2,1)} %bitcast.3, bf16[2048,128]{1,0:T(8,128)(2,1)} %wq_hbm.1, bf16[2048,128]{1,0:T(8,128)(2,1)} %wk_hbm.1, bf16[2048,1024]{1,0:T(8,128)(2,1)} %wv_hbm.1), custom_call_target="tpu_custom_call" | custom-call | tf_op jit(solution)/shard_map/pallas_call | solution.py:552
  82.4 2.1 %shard_map.85 = (bf16[1,128,2048]{2,1,0:T(8,128)(2,1)}, f32[64,128]{1,0:T(8,128)}, f32[64,128]{1,0:T(8,128)}, f32[64,1024]{1,0:T(8,128)}) custom-call(bf16[128,2048]{1,0:T(8,128)(2,1)} %get-tuple-element.6.gi_ref, f32[10,64,128]{2,1,0:T(8,128)} %get-tuple-element.7.o_ref), custom_call_target="tpu_custom_call" | custom-call | tf_op jit(solution)/shard_map/pallas_call | solution.py:577

commit v4 on v3

--- a/solution.py
+++ b/solution.py
@@ -19,6 +19,8 @@
 ROWS = HALF // PIECES
 BITS = (1, 2, 4)
 PLANE = 4
+LAGS = (0, 2, 4, 6, 8)
+LEAD = 3
 MESH = pl.DeviceIdType.MESH
 BF = jnp.bfloat16
 F32 = jnp.float32
@@ -184,6 +186,12 @@
         src = st.at[flip(r, k) % PLANE]
         shares.append(push(src, xg.at[r], xs.at[k], xr.at[k], mate(k)))
     xg[r] = st[r % PLANE]
+
+    def swap(k):
+        at = flip(r, k)
+        return push(xg.at[at], xp.at[at], ps.at[k], pr.at[k], (seq, other))
+
+    nears = [swap(0)]
 
     causal = lax.broadcasted_iota(jnp.int32, (span, span), 0) <= lax.broadcasted_iota(
         jnp.int32, (span, span), 1
@@ -307,13 +315,6 @@
         gvs[c] = gv
         gfks[c] = gfk
 
-    for copy in shares:
-        copy.wait_recv()
-    base = (r // PLANE) * PLANE
-    near = push(
-        xg.at[pl.ds(base, PLANE)], xp.at[pl.ds(base, PLANE)], ps.at[0], pr.at[0], (seq, other)
-    )
-
     collect(rsend, rrecv, rs, rr, -1, rin)
     in_values, in_norms = unpack(rin[...])
     in_pair, in_norm_pair = halves(in_values), halves(in_norms)
@@ -325,7 +326,8 @@
         store(c, HALF + DK, gv[DV // 2 :])
         store(c, HALF, pull(part(c, DK, DK) * 0.5, gfk) * 0.5)
 
-    pending = [near] + shares + ups + qkv
+    pending = shares + ups + qkv
+    base = (r // PLANE) * PLANE
     here = pl.ds(base, PLANE)
     there = pl.ds(PLANE - base, PLANE)
     place = r % PLANE
@@ -418,57 +420,85 @@
             )
         )
 
-    def combine(i):
-        for m in range(2):
-            landed(lr.at[i, m], br.at[i, m])
-            for a in range(ng):
-                acc[i, a, m] = ls[i, m, side, a] + lr[i, m, a]
+    def combine(i, m):
+        landed(lr.at[i, m], br.at[i, m])
+        for a in range(ng):
+            acc[i, m, a] = ls[i, m, side, a] + lr[i, m, a]
         for d in range(1, ng):
             to = (g + d) % ng
             pending.append(
-                push(acc.at[i, to], l2.at[i, d], cs.at[i, d], cr.at[i, d], (to * H + r, core))
+                push(
+                    acc.at[i, m, to], l2.at[i, m, d], cs.at[i, m, d], cr.at[i, m, d],
+                    (to * H + r, core),
+                )
             )
 
     swaps = []
 
     def settled(i):
-        total = acc[i, g]
-        for d in range(1, ng):
-            landed(l2.at[i, d], cr.at[i, d])
-            total = total + l2[i, d]
         for m in range(2):
+            total = acc[i, m, g]
+            for d in range(1, ng):
+                landed(l2.at[i, m, d], cr.at[i, m, d])
+                total = total + l2[i, m, d]
             for k in range(PLANE):
-                rows = total[m, k * ROWS : (k + 1) * ROWS]
-                f2[core, i, flip(mirror if m else r, k)] = rows
+                f2[core, i, flip(mirror if m else r, k)] = total[k * ROWS : (k + 1) * ROWS]
         swaps.append(push(f2.at[core, i], f2.at[core, i], ds.at[i], dr.at[i], (seq, other)))
 
-    across(0)
-    direct(0)
-    across(1)
-    direct(1)
-    for i in range(2, PIECES):
+    def spread(u):
+        if u < PIECES:
+            direct(u)
+        else:
+            mirrored(u - PIECES)
+
+    def relayed(u):
+        forward(u % PIECES, u // PIECES)
+
+    def product_of(u):
+        multiply(u % PIECES, u // PIECES)
+        if u >= PIECES:
+            combine(u - PIECES, 1)
+
+    def joined(u):
+        if u >= PIECES:
+            combine(u - PIECES, 0)
+
+    def done(u):
+        if u >= PIECES:
+            settled(u - PIECES)
+
+    units = 2 * PIECES
+    stages = list(zip((spread, relayed, product_of, joined, done), LAGS))
+
+    def run(begin, end, only):
+        for t in range(begin, end):
+            for n, (stage, lag) in enumerate(stages):
+                if n in only and 0 <= t - lag < units:
+                    stage(t - lag)
+
+    for i in range(PIECES):
         across(i)
+        if i < LEAD:
+            spread(i)
     for i in range(PIECES):
         gj[i, 0, 0, core] = o[here, core, i * ROWS : (i + 1) * ROWS, :]
-    near.wait_recv()
+    for k in range(1, PLANE):
+        shares[k - 1].wait_recv()
+        nears.append(swap(k))
+    pending += nears
+    relayed(0)
+    for copy in nears:
+        copy.wait_recv()
     for j in range(PLANE):
         xb[core, j * length : (j + 1) * length, :] = xg[base + j].astype(BF)
         xb[other, j * length : (j + 1) * length, :] = xp[base + j].astype(BF)
-    mirrored(0)
-    forward(0, 0)
-    for i in range(PIECES):
-        if i + 1 < PIECES:
-            mirrored(i + 1)
-            forward(i + 1, 0)
-        if i + 2 < PIECES:
-            direct(i + 2)
-        forward(i, 1)
-        multiply(i, 0)
-        multiply(i, 1)
-        if i > 0:
-            combine(i - 1)
-        if i > 1:
-            settled(i - 2)
+    every = range(5)
+    stop = units + LAGS[2]
+    first_turn = max(LEAD, LAGS[1] + 1)
+    if LEAD < first_turn:
+        run(LEAD, first_turn, (0,))
+    run(LAGS[1] + 1, LEAD, every[1:])
+    run(first_turn, stop, every)
     for i in range(PIECES):
         for m in range(2):
             landed(rt.at[other, i, m], tr.at[i, m])
@@ -492,20 +522,16 @@
         total = total + dot(jt[:, 2 * DV :], wv_ref[rows, :], (1, 1))
         gi_ref[:, rows] = total.astype(BF)
 
-    combine(PIECES - 1)
-    for i in range(PIECES - 2, PIECES):
-        settled(i)
+    run(stop, units + LAGS[4], every)
     for copy in swaps:
         copy.wait_recv()
-    final = [jnp.concatenate([f2[n, 0, h, :DK] for h in range(H)], 0) for n in range(2)]
+    whole = [
+        [jnp.concatenate([f2[n, i, h] for i in range(PIECES)], 0) for n in range(2)]
+        for h in range(H)
+    ]
+    final = [jnp.concatenate([whole[h][n][:DK] for h in range(H)], 0) for n in range(2)]
     for h in range(H):
-        parts = []
-        for n in range(2):
-            for i in range(PIECES):
-                start = max(DK - i * ROWS, 0)
-                if start < ROWS:
-                    parts.append(f2[n, i, h, start:])
-        final.append(jnp.concatenate(parts, 0))
+        final.append(jnp.concatenate([whole[h][0][DK:], whole[h][1][DK:]], 0))
     keep = owned // 2
     for n, block in enumerate(final):
         fs[n] = block.T
@@ -539,15 +565,15 @@
         vm(*state), vm(ng, *state), vm(*state), vm(*state), vm(ng, *state), vm(*state),
         vm(H, 2, HALF, length), vm(PIECES, 2, PLANE, 2, PLANE, ROWS, length),
         vm(PIECES, 2, 2, ng, PLANE * ROWS, owned), vm(PIECES, 2, ng, PLANE * ROWS, owned),
-        vm(PIECES, ng, 2, PLANE * ROWS, owned), vm(PIECES, ng, 2, PLANE * ROWS, owned),
+        vm(PIECES, 2, ng, PLANE * ROWS, owned), vm(PIECES, 2, ng, PLANE * ROWS, owned),
         vm(2, PIECES, 2, PLANE, ROWS, length), half(length, H * DV + 2 * DV),
         vm(2, PIECES, H, ROWS, owned), vm(2 + H, owned, DV),
         sems(5),
         sems(H), sems(H), sems(H), sems(H), sems(PLANE), sems(PLANE),
-        sems(1), sems(1), sems(ng), sems(ng), sems(ng), sems(ng),
+        sems(PLANE), sems(PLANE), sems(ng), sems(ng), sems(ng), sems(ng),
         sems(PIECES, 2), sems(PIECES, 2, PLANE, 2), sems(PIECES, 2, PLANE, 2), sems(PIECES, 2),
         sems(PIECES, 2), sems(PIECES, 2), sems(PIECES, 2), sems(PIECES, 2),
-        sems(PIECES, ng), sems(PIECES, ng), sems(PIECES), sems(PIECES),
+        sems(PIECES, 2, ng), sems(PIECES, 2, ng), sems(PIECES), sems(PIECES),
     ]
     return pl.pallas_call(
         functools.partial(fused_kernel, ng),

time: 84.9 us -> 74.5 us (0.88)
  Pallas kernels: 83.8 us -> 72.8 us
    pallas_call x1, Pallas kernels: 81.8 us -> 70.8 us  [fused(): pl.pallas_call(functools.partial(fused_kernel, ng), out_shape=[jax.ShapeD...]
where the time goes in v4:
time: 74.5 us; the launch traced here: 73.5 us
  Pallas kernels  72.8 us (98%)
    pallas_call x1, Pallas kernels, fused(): pl.pallas_call(functools.partial(fused_kernel, ng), out_shape=[jax.ShapeD...  70.8 us
    pallas_call x1, Pallas kernels, finish(): pl.pallas_call(finish_kernel, out_shape=[jax.ShapeDtypeStruct((1,) + grad...  2.06 us

profile of v4, /device:TPU:0, one launch (start us, length us, event | category | flops | bytes accessed | tf_op | source)
XLA Modules:
  0.0 73.5 jit_solution(7906822998570630580)
XLA Ops:
  0.6 70.8 %shard_map.84 = (bf16[128,2048]{1,0:T(8,128)(2,1)}, f32[10,64,128]{2,1,0:T(8,128)}) custom-call(bf16[128,2048]{1,0:T(8,128)(2,1)} %bitcast.2, bf16[128,1024]{1,0:T(8,128)(2,1)} %bitcast.3, bf16[2048,128]{1,0:T(8,128)(2,1)} %wq_hbm.1, bf16[2048,128]{1,0:T(8,128)(2,1)} %wk_hbm.1, bf16[2048,1024]{1,0:T(8,128)(2,1)} %wv_hbm.1), custom_call_target="tpu_custom_call" | custom-call | tf_op jit(solution)/shard_map/pallas_call | solution.py:578
  71.4 2.1 %shard_map.85 = (bf16[1,128,2048]{2,1,0:T(8,128)(2,1)}, f32[64,128]{1,0:T(8,128)}, f32[64,128]{1,0:T(8,128)}, f32[64,1024]{1,0:T(8,128)}) custom-call(bf16[128,2048]{1,0:T(8,128)(2,1)} %get-tuple-element.6.gi_ref, f32[10,64,128]{2,1,0:T(8,128)} %get-tuple-element.7.o_ref), custom_call_target="tpu_custom_call" | custom-call | tf_op jit(solution)/shard_map/pallas_call | solution.py:603

commit v5 on v4

--- a/solution.py
+++ b/solution.py
@@ -19,7 +19,7 @@
 ROWS = HALF // PIECES
 BITS = (1, 2, 4)
 PLANE = 4
-LAGS = (0, 2, 4, 6, 8)
+LAGS = (0, 2, 4, 7, 10)
 LEAD = 3
 MESH = pl.DeviceIdType.MESH
 BF = jnp.bfloat16
@@ -112,11 +112,11 @@
 
 
 def fused_kernel(
-    ng, x_hbm, c_hbm, wq_hbm, wk_hbm, wv_hbm, gi_ref, out_ref,
-    x_ref, c_ref, wq_ref, wk_ref, wv_ref, own, rec, st, xg, xp, xb,
+    ng, x_hbm, c_hbm, wq_hbm, wk_hbm, wv_hbm, gi_hbm, out_ref,
+    gi_ref, x_ref, c_ref, wq_ref, wk_ref, wv_ref, own, rec, st, xg, xp, xb,
     fqs, fks, vas, ah, al, nh, nl, tops, pv, rv, gvs, gfks,
     ssend, srecv, sin, rsend, rrecv, rin, o, gj, ls, lr, acc, l2, rt, jt, f2, fs,
-    load, us, ur, qs, qr, xs, xr, ps, pr, ss, sr, rs, rr,
+    load, save, us, ur, qs, qr, xs, xr, ps, pr, ss, sr, rs, rr,
     zs, gs, gr, hs, ts, tr, bs, br, cs, cr, ds, dr,
 ):
     seq = lax.axis_index("seq")
@@ -445,27 +445,36 @@
                 f2[core, i, flip(mirror if m else r, k)] = total[k * ROWS : (k + 1) * ROWS]
         swaps.append(push(f2.at[core, i], f2.at[core, i], ds.at[i], dr.at[i], (seq, other)))
 
+    order = [(0, 0)]
+    for i in range(1, PIECES):
+        order += [(i, 0), (i - 1, 1)]
+    order.append((PIECES - 1, 1))
+
     def spread(u):
-        if u < PIECES:
-            direct(u)
+        i, m = order[u]
+        if m == 0:
+            direct(i)
         else:
-            mirrored(u - PIECES)
+            mirrored(i)
 
     def relayed(u):
-        forward(u % PIECES, u // PIECES)
+        forward(*order[u])
 
     def product_of(u):
-        multiply(u % PIECES, u // PIECES)
-        if u >= PIECES:
-            combine(u - PIECES, 1)
+        i, m = order[u]
+        multiply(i, m)
+        if m == 1:
+            combine(i, 1)
 
     def joined(u):
-        if u >= PIECES:
-            combine(u - PIECES, 0)
+        i, m = order[u]
+        if m == 1:
+            combine(i, 0)
 
     def done(u):
-        if u >= PIECES:
-            settled(u - PIECES)
+        i, m = order[u]
+        if m == 1:
+            settled(i)
 
     units = 2 * PIECES
     stages = list(zip((spread, relayed, product_of, joined, done), LAGS))
@@ -499,6 +508,8 @@
         run(LEAD, first_turn, (0,))
     run(LAGS[1] + 1, LEAD, every[1:])
     run(first_turn, stop, every)
+    for u in range(stop - LAGS[3], units - 1):
+        joined(u)
     for i in range(PIECES):
         for m in range(2):
             landed(rt.at[other, i, m], tr.at[i, m])
@@ -514,15 +525,27 @@
         blocks.append(jnp.concatenate([whole[h][0][DK:], whole[h][1][DK:]], 0))
     for n, block in enumerate(blocks):
         jt[:, n * DV : (n + 1) * DV] = block.T.astype(BF)
-    step = 512
-    for at in range(0, width, step):
-        rows = slice(at, at + step)
-        total = dot(jt[:, :DV], wq_ref[rows, :], (1, 1))
-        total = total + dot(jt[:, DV : 2 * DV], wk_ref[rows, :], (1, 1))
-        total = total + dot(jt[:, 2 * DV :], wv_ref[rows, :], (1, 1))
-        gi_ref[:, rows] = total.astype(BF)
-
-    run(stop, units + LAGS[4], every)
+    stores = []
+
+    def flow(begin, end, step):
+        for at in range(begin, end, step):
+            rows = slice(at, at + step)
+            total = dot(jt[:, :DV], wq_ref[rows, :], (1, 1))
+            total = total + dot(jt[:, DV : 2 * DV], wk_ref[rows, :], (1, 1))
+            total = total + dot(jt[:, 2 * DV :], wv_ref[rows, :], (1, 1))
+            gi_ref[:, rows] = total.astype(BF)
+            copy = pltpu.make_async_copy(
+                gi_ref.at[:, rows], gi_hbm.at[:, rows], save.at[at // step]
+            )
+            copy.start()
+            stores.append(copy)
+
+    flow(0, width // 2, width // 4)
+    joined(units - 1)
+    flow(width // 2, width, width // 4)
+
+    for u in range(stop - LAGS[4], units):
+        done(u)
     for copy in swaps:
         copy.wait_recv()
     whole = [
@@ -539,6 +562,8 @@
     pending += swaps
     for copy in pending:
         copy.wait_send()
+    for copy in stores:
+        copy.wait()
     settle(ssend, srecv, ss, sr, 1)
     settle(rsend, rrecv, rs, rr, -1)
 
@@ -551,7 +576,7 @@
     vm = lambda *shape: pltpu.VMEM(shape, F32)
     half = lambda *shape: pltpu.VMEM(shape, BF)
     state = (FEATS + 16, DV)
-    scratch = [half(length, width), half(length, H * DV)]
+    scratch = [half(length, width), half(length, width), half(length, H * DV)]
     scratch += [pltpu.VMEM(w.shape, w.dtype) for w in weights]
     scratch += [
         vm(H, 2 * DK + 2 * DV, length), vm(H, 2 * DK + 2 * DV, length),
@@ -568,7 +593,7 @@
         vm(PIECES, 2, ng, PLANE * ROWS, owned), vm(PIECES, 2, ng, PLANE * ROWS, owned),
         vm(2, PIECES, 2, PLANE, ROWS, length), half(length, H * DV + 2 * DV),
         vm(2, PIECES, H, ROWS, owned), vm(2 + H, owned, DV),
-        sems(5),
+        sems(5), sems(4),
         sems(H), sems(H), sems(H), sems(H), sems(PLANE), sems(PLANE),
         sems(PLANE), sems(PLANE), sems(ng), sems(ng), sems(ng), sems(ng),
         sems(PIECES, 2), sems(PIECES, 2, PLANE, 2), sems(PIECES, 2, PLANE, 2), sems(PIECES, 2),
@@ -582,7 +607,7 @@
             jax.ShapeDtypeStruct((2 + H, owned // 2, DV), F32),
         ],
         in_specs=[HBM] * 5,
-        out_specs=[VMEM] * 2,
+        out_specs=[HBM, VMEM],
         scratch_shapes=scratch,
         compiler_params=pltpu.CompilerParams(
             collective_id=0, has_side_effects=True, vmem_limit_bytes=60 << 20
@@ -590,16 +615,40 @@
     )(tokens, upstream, *weights)
 
 
-def finish_kernel(gi_ref, o_ref, in_ref, oq_ref, ok_ref, ov_ref):
-    in_ref[0] = gi_ref[...]
-    oq_ref[...] = o_ref[0]
-    ok_ref[...] = o_ref[1]
+def finish_kernel(gi_ref, o_ref, in_ref, oq_ref, ok_ref, ov_ref, grad, held, into, out):
+    parts = into.shape[0] - 1
+    rows = gi_ref.shape[0] // parts
+    loads = [pltpu.make_async_copy(o_ref, held, into.at[parts])]
+    for n in range(parts):
+        at = pl.ds(n * rows, rows)
+        loads.append(pltpu.make_async_copy(gi_ref.at[at], grad.at[at], into.at[n]))
+    for copy in loads:
+        copy.start()
+    loads[0].wait()
+    stores = [
+        pltpu.make_async_copy(held.at[0], oq_ref, out.at[0]),
+        pltpu.make_async_copy(held.at[1], ok_ref, out.at[1]),
+    ]
     for n in range(H):
-        ov_ref[:, n * DV : (n + 1) * DV] = o_ref[2 + n]
+        columns = pl.ds(n * DV, DV)
+        stores.append(
+            pltpu.make_async_copy(held.at[2 + n], ov_ref.at[:, columns], out.at[2 + n])
+        )
+    for copy in stores:
+        copy.start()
+    for n in range(parts):
+        at = pl.ds(n * rows, rows)
+        loads[1 + n].wait()
+        copy = pltpu.make_async_copy(grad.at[at], in_ref.at[0, at], out.at[2 + H + n])
+        copy.start()
+        stores.append(copy)
+    for copy in stores:
+        copy.wait()
 
 
 def finish(grad_in, blocks):
     _, rows, lanes = blocks.shape
+    parts = 4
     return pl.pallas_call(
         finish_kernel,
         out_shape=[
@@ -608,8 +657,14 @@
             jax.ShapeDtypeStruct((rows, lanes), F32),
             jax.ShapeDtypeStruct((rows, H * lanes), F32),
         ],
-        in_specs=[VMEM] * 2,
-        out_specs=[VMEM] * 4,
+        in_specs=[HBM] * 2,
+        out_specs=[HBM] * 4,
+        scratch_shapes=[
+            pltpu.VMEM(grad_in.shape, BF),
+            pltpu.VMEM(blocks.shape, F32),
+            sems(1 + parts),
+            sems(2 + H + parts),
+        ],
     )(grad_in, blocks)
 
 

time: 74.5 us -> 74 us (level)
  no operation moved by 1% of the time
where the time goes in v5:
time: 74 us; the launch traced here: 73.4 us
  Pallas kernels  72.7 us (98%)
    pallas_call x1, Pallas kernels, fused(): pl.pallas_call(functools.partial(fused_kernel, ng), out_shape=[jax.ShapeD...  70.7 us
    pallas_call x1, Pallas kernels, finish(): pl.pallas_call(finish_kernel, out_shape=[jax.ShapeDtypeStruct((1,) + grad...  2.03 us

profile of v5, /device:TPU:0, one launch (start us, length us, event | category | flops | bytes accessed | tf_op | source)
XLA Modules:
  0.0 73.4 jit_solution(16593295555058801462)
XLA Ops:
  0.6 70.7 %shard_map.84 = (bf16[128,2048]{1,0:T(8,128)(2,1)}, f32[10,64,128]{2,1,0:T(8,128)}) custom-call(bf16[128,2048]{1,0:T(8,128)(2,1)} %bitcast.2, bf16[128,1024]{1,0:T(8,128)(2,1)} %bitcast.3, bf16[2048,128]{1,0:T(8,128)(2,1)} %wq_hbm.1, bf16[2048,128]{1,0:T(8,128)(2,1)} %wk_hbm.1, bf16[2048,1024]{1,0:T(8,128)(2,1)} %wv_hbm.1), custom_call_target="tpu_custom_call" | custom-call | tf_op jit(solution)/shard_map/pallas_call | solution.py:603
  71.4 2.0 %shard_map.85 = (bf16[1,128,2048]{2,1,0:T(8,128)(2,1)}, f32[64,128]{1,0:T(8,128)}, f32[64,128]{1,0:T(8,128)}, f32[64,1024]{1,0:T(8,128)}) custom-call(bf16[128,2048]{1,0:T(8,128)(2,1)} %get-tuple-element.6.gi_ref, f32[10,64,128]{2,1,0:T(8,128)} %get-tuple-element.7.o_ref), custom_call_target="tpu_custom_call" | custom-call | tf_op jit(solution)/shard_map/pallas_call | solution.py:652

commit v6 on v5

--- a/solution.py
+++ b/solution.py
@@ -233,17 +233,15 @@
                 ).wait_recv()
                 total[...] += dst[d]
 
-    for copy in ups + qkv:
+    for copy in qkv:
         copy.wait_recv()
 
     values = jnp.zeros((FEATS, DV), F32)
     norms = jnp.zeros((AUX, FEATS), F32)
     norm_at = []
     for c in range(chunks):
-        fq = phi(part(c, 0, DK) * 0.5).astype(BF)
         fk = phi(part(c, DK, DK) * 0.5).astype(BF)
         va = jnp.concatenate([part(c, 2 * DK, DV), ones], 0).astype(BF)
-        fqs[c] = fq
         fks[c] = fk
         vas[c] = va
         pv[c] = values
@@ -254,7 +252,9 @@
     relay(ssend, srecv, ss, sr, 1)
 
     for c in range(chunks):
-        fq, fk, va = fqs[c], fks[c], vas[c]
+        fq = phi(part(c, 0, DK) * 0.5).astype(BF)
+        fqs[c] = fq
+        fk, va = fks[c], vas[c]
         attn = halves(jnp.where(causal, dot(fk, fq, (0, 0)), 0.0))
         ah[c] = attn[0]
         al[c] = attn[1]
@@ -266,6 +266,8 @@
         tops[c] = top
 
     collect(ssend, srecv, ss, sr, 1, sin)
+    for copy in ups:
+        copy.wait_recv()
     in_values, in_norms = unpack(sin[...])
     in_pair, in_norm_pair = halves(in_values), halves(in_norms)
     back = jnp.zeros((FEATS, DV), F32)

time: 74 us -> 74 us (level)
  no operation moved by 1% of the time
where the time goes in v6:
time: 74 us; the launch traced here: 73.4 us
  Pallas kernels  72.7 us (98%)
    pallas_call x1, Pallas kernels, fused(): pl.pallas_call(functools.partial(fused_kernel, ng), out_shape=[jax.ShapeD...  70.7 us
    pallas_call x1, Pallas kernels, finish(): pl.pallas_call(finish_kernel, out_shape=[jax.ShapeDtypeStruct((1,) + grad...  2.03 us

profile of v6, /device:TPU:0, one launch (start us, length us, event | category | flops | bytes accessed | tf_op | source)
XLA Modules:
  0.0 73.4 jit_solution(5363579305751703154)
XLA Ops:
  0.6 70.7 %shard_map.84 = (bf16[128,2048]{1,0:T(8,128)(2,1)}, f32[10,64,128]{2,1,0:T(8,128)}) custom-call(bf16[128,2048]{1,0:T(8,128)(2,1)} %bitcast.2, bf16[128,1024]{1,0:T(8,128)(2,1)} %bitcast.3, bf16[2048,128]{1,0:T(8,128)(2,1)} %wq_hbm.1, bf16[2048,128]{1,0:T(8,128)(2,1)} %wk_hbm.1, bf16[2048,1024]{1,0:T(8,128)(2,1)} %wv_hbm.1), custom_call_target="tpu_custom_call" | custom-call | tf_op jit(solution)/shard_map/pallas_call | solution.py:605
  71.3 2.0 %shard_map.85 = (bf16[1,128,2048]{2,1,0:T(8,128)(2,1)}, f32[64,128]{1,0:T(8,128)}, f32[64,128]{1,0:T(8,128)}, f32[64,1024]{1,0:T(8,128)}) custom-call(bf16[128,2048]{1,0:T(8,128)(2,1)} %get-tuple-element.6.gi_ref, f32[10,64,128]{2,1,0:T(8,128)} %get-tuple-element.7.o_ref), custom_call_target="tpu_custom_call" | custom-call | tf_op jit(solution)/shard_map/pallas_call | solution.py:654
